TPU v7x, 256 devices: a whole 4x4x8 slice. The times are simulated.
256 devices in a mesh: sta: 16 (over x_hi, y, core), cel: 16 (over x_lo, z).
Axes of the slice: x: 4 (x_hi: 2, x_lo: 2; x = x_hi * 2 + x_lo), y: 4, z: 8, core: 2. Of those that a mesh axis runs over, the one named last changes fastest.
Arguments:
- station_plane: int32 [2, 65536], P(None, 'sta'), may hold values from 0 to 191
- station_height: int32 [65536], P('sta'), may hold values from 1 to 4
- cell_plane: int32 [2, 32768], P(None, 'cel'), may hold values from 0 to 191
- cell_depth: int32 [32768], P('cel'), may hold values from 0 to 15
- cell_density: float32 [32768], P('cel'), may hold values from 0.4 to 4
- left_before: float32 [16, 65536], P(None, 'sta'), may hold values from -6 to 6
- left_now: float32 [16, 65536], P(None, 'sta'), may hold values from -6 to 6
- right_before: float32 [16, 32768], P(None, 'cel'), may hold values from -6 to 6
Outputs:
- right_blocks: float32 [2, 16, 32768], P(None, None, 'cel')
- left_block: float32 [16, 65536], P(None, 'sta')
- alphas: float32 [2, 16, 16], replicated
- betas: float32 [2, 16, 16], replicated
All inputs are finite; a program needn't handle non-finite values.
Results may differ from a plain program's by a relative error of at most 0.0003.
Values sent between devices are 32-bit elements; how exact they have to be, the bound alone decides.
No kernel may reach another device: no remote copies, remote signals or barrier semaphores. Data moves between devices by JAX's collectives and lax.ppermute only.
A program may use at most 64 MiB of HBM per device.

v0:
```python
import jax
import jax.numpy as jnp
from jax import lax
from jax.sharding import PartitionSpec as P

STEPS = 2


GAIN = 4.0
HIGH = lax.Precision.HIGHEST


def sent_to_all(value, axis):
    copies = jnp.broadcast_to(value, (lax.axis_size(axis), *value.shape))
    return lax.all_to_all(copies, axis, split_axis=0, concat_axis=0, tiled=True)


def of_everyone(value, axis):
    return sent_to_all(value, axis).sum(axis=0)


def filled_up(lines, length):
    spare = -len(lines) % length
    return jnp.pad(lines, [(0, spare)] + [(0, 0)] * (lines.ndim - 1))


def in_order(blocks, dim):
    dims = list(blocks.shape[1:])
    dims[dim] *= blocks.shape[0]
    return jnp.moveaxis(blocks, 0, dim).reshape(dims)


def collect(value, axis, dim):
    blocks = sent_to_all(value, axis)
    return in_order(blocks, dim)


def cut_along(value, dim, length):
    before, after = (value.shape[:dim], value.shape[dim + 1 :])
    return jnp.moveaxis(value.reshape(*before, length, -1, *after), dim, 0)


def sent_and_summed(value, axis, dim):
    length = lax.axis_size(axis)
    blocks = lax.all_to_all(cut_along(value, dim, length), axis, 0, 0, tiled=True)
    return jnp.sum(blocks, axis=0)


def total_of(value, axes):
    lines = value.reshape(-1, value.shape[-1])
    padded = filled_up(lines, lax.axis_size(axes))
    whole = collect(sent_and_summed(padded, axes, 0), axes, 0)
    return lax.slice_in_dim(whole, 0, len(lines)).reshape(value.shape)


def kernel_rows(sx, sy, sz, cx, cy, cz, density):
    dx = sx[:, None] - cx[None, :]
    dy = sy[:, None] - cy[None, :]
    dz = sz[:, None] + cz[None, :] + 0.5
    square = dx * dx + dy * dy + dz * dz
    inverse = lax.rsqrt(square)
    inv_two = inverse * inverse
    return (
        GAIN
        * density[None, :]
        * (2.0 * dz * dz - dx * dx - dy * dy)
        * (inv_two * inv_two * inverse)
    )


def matmul(a, b):
    return jnp.dot(a, b, precision=HIGH, preferred_element_type=jnp.float32)


def cell_sum(values):
    return of_everyone(values, "cel")


def station_sum(values):
    return of_everyone(values, "sta")


def orthonormal(block, basis, rows, summer):
    coef = summer(matmul(basis, block.T)) / rows
    rest = block - matmul(coef.T, basis)
    gram = summer(matmul(rest, rest.T)) / rows
    lower = jnp.linalg.cholesky(gram)
    return (jax.scipy.linalg.solve_triangular(lower, rest, lower=True), lower)


def body(
    station_plane,
    station_height,
    cell_plane,
    cell_depth,
    cell_density,
    left_before,
    left_now,
    right_before,
):
    width = left_now.shape[0]
    s_dev = left_now.shape[1]
    c_dev = right_before.shape[1]
    n_sta = lax.axis_size("sta")
    n_cel = lax.axis_size("cel")
    stations = s_dev * n_sta
    cells = c_dev * n_cel
    sx = station_plane[0].astype(jnp.float32)
    sy = station_plane[1].astype(jnp.float32)
    sz = station_height.astype(jnp.float32)
    cx = cell_plane[0].astype(jnp.float32)
    cy = cell_plane[1].astype(jnp.float32)
    cz = cell_depth.astype(jnp.float32)
    block = 512
    count = s_dev // block

    def tile_at(start):
        a = lax.dynamic_slice_in_dim(sx, start, block)
        b = lax.dynamic_slice_in_dim(sy, start, block)
        c = lax.dynamic_slice_in_dim(sz, start, block)
        return kernel_rows(a, b, c, cx, cy, cz, cell_density)

    right_basis = right_before
    left_basis = jnp.concatenate([left_before, left_now], 0)
    left = left_now
    rights, alphas, betas = ([], [], [])
    for step in range(STEPS):

        def add_block(index, total):
            start = index * block
            rows = lax.dynamic_slice_in_dim(left, start, block, 1)
            return total + matmul(rows, tile_at(start))

        adjoint_terms = lax.fori_loop(0, count, add_block, jnp.zeros((width, c_dev), jnp.float32))
        whole = total_of(adjoint_terms, "sta")
        right, alpha = orthonormal(whole, right_basis, cells, cell_sum)
        right_basis = jnp.concatenate([right_basis, right], 0)

        def one_block(index):
            return lax.dot_general(
                right,
                tile_at(index * block),
                (((1,), (1,)), ((), ())),
                precision=HIGH,
                preferred_element_type=jnp.float32,
            )

        parts = lax.map(one_block, jnp.arange(count))
        forward_terms = parts.transpose(1, 0, 2).reshape(width, s_dev)
        whole_left = total_of(forward_terms, "cel")
        left, beta = orthonormal(whole_left, left_basis, stations, station_sum)
        left_basis = jnp.concatenate([left_basis, left], 0)
        rights.append(right)
        alphas.append(alpha)
        betas.append(beta)
    return (jnp.stack(rights), left, jnp.stack(alphas), jnp.stack(betas))


def solution(mesh):
    in_specs = (
        P(None, "sta"),
        P("sta"),
        P(None, "cel"),
        P("cel"),
        P("cel"),
        P(None, "sta"),
        P(None, "sta"),
        P(None, "cel"),
    )
    out_specs = (P(None, None, "cel"), P(None, "sta"), P(), P())
    return jax.shard_map(body, mesh=mesh, in_specs=in_specs, out_specs=out_specs, check_vma=False)
```

profile of v0, /device:TPU:1, one launch (start us, length us, event | category | flops | bytes accessed | tf_op | source)
XLA Modules:
  0.0 452.6 jit_solution(2137172877894747576)
XLA Ops:
  3.7 51.1 %while.50 = (s32[]{:T(128)}, f32[16,2048]{1,0:T(8,128)S(1)}, f32[16,4096]{1,0:T(8,128)}, f32[2048]{0:T(1024)}, f32[4096]{0:T(1024)S(1)}, /*index=5*/f32[2048]{0:...) while((s32[]{:T(128)}, f32[16,2048]{1,0:T(8,128)S(1)}, ...), condition=%wide.region_1.0_spmd.clone, body=%wide.region_0.0_spmd.clone.sunk | while | flops 220268544 | bytes 362709 | solution.py:134
  4.7 5.5 %fusion.228 = f32[16,2048]{1,0:T(8,128)S(1)} fusion(f32[2048]{0:T(1024)S(1)} %get-tuple-element.918, f32[512]{0:T(512)S(1)} %dynamic_slice.118, f32[2048]{0:T(1024)S(1)} %get-tuple-element.916, f32[512]{0:T(512)S(1)} %dynamic_slice.119, f32[2048]{0:T(1024)S(1)} %get-tuple-element.914, f32[512]{0:T(512)S(1)} %dynamic_slice.120, ...), kind=kOutput, calls=%fused_computation.85.clone.1 | convolution fusion | flops 220266496 | bytes 333829 | tf_op jit(solution)/shard_map/while/body/eval_jaxpr/dot_general | solution.py:72
  11.1 5.5 %fusion.228 = f32[16,2048]{1,0:T(8,128)S(1)} fusion(f32[2048]{0:T(1024)S(1)} %get-tuple-element.918, f32[512]{0:T(512)S(1)} %dynamic_slice.118, f32[2048]{0:T(1024)S(1)} %get-tuple-element.916, f32[512]{0:T(512)S(1)} %dynamic_slice.119, f32[2048]{0:T(1024)S(1)} %get-tuple-element.914, f32[512]{0:T(512)S(1)} %dynamic_slice.120, ...), kind=kOutput, calls=%fused_computation.85.clone.1 | convolution fusion | flops 220266496 | bytes 333829 | tf_op jit(solution)/shard_map/while/body/eval_jaxpr/dot_general | solution.py:72
  17.5 5.5 %fusion.228 = f32[16,2048]{1,0:T(8,128)S(1)} fusion(f32[2048]{0:T(1024)S(1)} %get-tuple-element.918, f32[512]{0:T(512)S(1)} %dynamic_slice.118, f32[2048]{0:T(1024)S(1)} %get-tuple-element.916, f32[512]{0:T(512)S(1)} %dynamic_slice.119, f32[2048]{0:T(1024)S(1)} %get-tuple-element.914, f32[512]{0:T(512)S(1)} %dynamic_slice.120, ...), kind=kOutput, calls=%fused_computation.85.clone.1 | convolution fusion | flops 220266496 | bytes 333829 | tf_op jit(solution)/shard_map/while/body/eval_jaxpr/dot_general | solution.py:72
  23.8 5.5 %fusion.228 = f32[16,2048]{1,0:T(8,128)S(1)} fusion(f32[2048]{0:T(1024)S(1)} %get-tuple-element.918, f32[512]{0:T(512)S(1)} %dynamic_slice.118, f32[2048]{0:T(1024)S(1)} %get-tuple-element.916, f32[512]{0:T(512)S(1)} %dynamic_slice.119, f32[2048]{0:T(1024)S(1)} %get-tuple-element.914, f32[512]{0:T(512)S(1)} %dynamic_slice.120, ...), kind=kOutput, calls=%fused_computation.85.clone.1 | convolution fusion | flops 220266496 | bytes 333829 | tf_op jit(solution)/shard_map/while/body/eval_jaxpr/dot_general | solution.py:72
  30.2 5.5 %fusion.228 = f32[16,2048]{1,0:T(8,128)S(1)} fusion(f32[2048]{0:T(1024)S(1)} %get-tuple-element.918, f32[512]{0:T(512)S(1)} %dynamic_slice.118, f32[2048]{0:T(1024)S(1)} %get-tuple-element.916, f32[512]{0:T(512)S(1)} %dynamic_slice.119, f32[2048]{0:T(1024)S(1)} %get-tuple-element.914, f32[512]{0:T(512)S(1)} %dynamic_slice.120, ...), kind=kOutput, calls=%fused_computation.85.clone.1 | convolution fusion | flops 220266496 | bytes 333829 | tf_op jit(solution)/shard_map/while/body/eval_jaxpr/dot_general | solution.py:72
  36.6 5.5 %fusion.228 = f32[16,2048]{1,0:T(8,128)S(1)} fusion(f32[2048]{0:T(1024)S(1)} %get-tuple-element.918, f32[512]{0:T(512)S(1)} %dynamic_slice.118, f32[2048]{0:T(1024)S(1)} %get-tuple-element.916, f32[512]{0:T(512)S(1)} %dynamic_slice.119, f32[2048]{0:T(1024)S(1)} %get-tuple-element.914, f32[512]{0:T(512)S(1)} %dynamic_slice.120, ...), kind=kOutput, calls=%fused_computation.85.clone.1 | convolution fusion | flops 220266496 | bytes 333829 | tf_op jit(solution)/shard_map/while/body/eval_jaxpr/dot_general | solution.py:72
  43.0 5.5 %fusion.228 = f32[16,2048]{1,0:T(8,128)S(1)} fusion(f32[2048]{0:T(1024)S(1)} %get-tuple-element.918, f32[512]{0:T(512)S(1)} %dynamic_slice.118, f32[2048]{0:T(1024)S(1)} %get-tuple-element.916, f32[512]{0:T(512)S(1)} %dynamic_slice.119, f32[2048]{0:T(1024)S(1)} %get-tuple-element.914, f32[512]{0:T(512)S(1)} %dynamic_slice.120, ...), kind=kOutput, calls=%fused_computation.85.clone.1 | convolution fusion | flops 220266496 | bytes 333829 | tf_op jit(solution)/shard_map/while/body/eval_jaxpr/dot_general | solution.py:72
  49.4 5.5 %fusion.228 = f32[16,2048]{1,0:T(8,128)S(1)} fusion(f32[2048]{0:T(1024)S(1)} %get-tuple-element.918, f32[512]{0:T(512)S(1)} %dynamic_slice.118, f32[2048]{0:T(1024)S(1)} %get-tuple-element.916, f32[512]{0:T(512)S(1)} %dynamic_slice.119, f32[2048]{0:T(1024)S(1)} %get-tuple-element.914, f32[512]{0:T(512)S(1)} %dynamic_slice.120, ...), kind=kOutput, calls=%fused_computation.85.clone.1 | convolution fusion | flops 220266496 | bytes 333829 | tf_op jit(solution)/shard_map/while/body/eval_jaxpr/dot_general | solution.py:72
  55.6 8.4 %all-to-all-start = ((f32[16,1,2048]{2,1,0:T(1,128)}), f32[16,1,2048]{2,1,0:T(1,128)S(1)}, u32[]{:S(2)}, u32[]{:S(2)}) async-start(f32[16,1,2048]{2,1,0:T(1,128)} %reshape.111), calls=%async_computation | async-start | bytes 262144 | tf_op jit(solution)/shard_map/all_to_all | solution.py:45
  64.0 7.6 %all-to-all-done = f32[16,1,2048]{2,1,0:T(1,128)S(1)} async-done(((f32[16,1,2048]{2,1,0:T(1,128)}), f32[16,1,2048]{2,1,0:T(1,128)S(1)}, u32[]{:S(2)}, u32[]{:S(2)}) %all-to-all-start) | async-done | bytes 131104 | tf_op jit(solution)/shard_map/all_to_all | solution.py:45
  71.8 10.8 %all_to_all.80 = f32[16,1,2048]{2,1,0:T(1,128)S(1)} all-to-all(f32[16,1,2048]{2,1,0:T(1,128)S(1)} %broadcast_in_dim.100), channel_id=1, replica_groups=mesh['sta'=16,'cel'=16] {'sta'}, dimensions={0} | all-to-all | bytes 262144 | tf_op jit(solution)/shard_map/all_to_all | solution.py:15
  83.1 15.5 %all_to_all.84 = f32[16,1,256]{2,1,0:T(1,128)S(1)} all-to-all(f32[16,1,256]{2,1,0:T(1,128)S(1)} %reshape.121), channel_id=1, replica_groups=mesh['sta'=16,'cel'=16] {'cel'}, dimensions={0} | all-to-all | bytes 32768 | tf_op jit(solution)/shard_map/all_to_all | solution.py:15
  105.2 7.1 %all-to-all-done.3 = f32[16,1,256]{2,1,0:T(1,128)S(1)} async-done(((f32[16,1,256]{2,1,0:T(1,128)}), f32[16,1,256]{2,1,0:T(1,128)S(1)}, u32[]{:S(2)}, u32[]{:S(2)}) %all-to-all-start.3) | async-done | bytes 16416 | tf_op jit(solution)/shard_map/all_to_all | solution.py:15
  117.7 61.5 %while.48 = (s32[]{:T(128)}, f32[8,16,512]{2,1,0:T(8,128)S(1)}, f32[2048]{0:T(1024)S(1)}, s32[8]{0:T(128)S(1)}, f32[4096]{0:T(1024)S(1)}, /*index=5*/f32[2048]{0...) while((s32[]{:T(128)}, f32[8,16,512]{2,1,0:T(8,128)S(1)}, ...), condition=%wide.region_8.11_spmd, body=%wide.region_7.10_spmd.sunk | while | flops 220203008 | bytes 231647 | solution.py:148
  119.2 6.2 %fusion.222 = f32[8,16,512]{2,1,0:T(8,128)S(1)} fusion(f32[8,16,512]{2,1,0:T(8,128)S(1)} %get-tuple-element.939, s32[]{:T(128)S(6)} %copy.91, f32[16,2048]{1,0:T(8,128)S(1)} %get-tuple-element.963, f32[2048]{0:T(1024)S(1)} %get-tuple-element.962, f32[512]{0:T(512)S(1)} %dynamic_slice.110, f32[2048]{0:T(1024)S(1)} %get-tuple-element.960, ...), kind=kOutput, calls=%fused_computation.29.clone.1 | convolution fusion | flops 220200960 | bytes 202756 | tf_op jit(solution)/shard_map/while/body/eval_jaxpr/dot_general | solution.py:140
  126.9 6.2 %fusion.222 = f32[8,16,512]{2,1,0:T(8,128)S(1)} fusion(f32[8,16,512]{2,1,0:T(8,128)S(1)} %get-tuple-element.939, s32[]{:T(128)S(6)} %copy.91, f32[16,2048]{1,0:T(8,128)S(1)} %get-tuple-element.963, f32[2048]{0:T(1024)S(1)} %get-tuple-element.962, f32[512]{0:T(512)S(1)} %dynamic_slice.110, f32[2048]{0:T(1024)S(1)} %get-tuple-element.960, ...), kind=kOutput, calls=%fused_computation.29.clone.1 | convolution fusion | flops 220200960 | bytes 202756 | tf_op jit(solution)/shard_map/while/body/eval_jaxpr/dot_general | solution.py:140
  134.6 6.2 %fusion.222 = f32[8,16,512]{2,1,0:T(8,128)S(1)} fusion(f32[8,16,512]{2,1,0:T(8,128)S(1)} %get-tuple-element.939, s32[]{:T(128)S(6)} %copy.91, f32[16,2048]{1,0:T(8,128)S(1)} %get-tuple-element.963, f32[2048]{0:T(1024)S(1)} %get-tuple-element.962, f32[512]{0:T(512)S(1)} %dynamic_slice.110, f32[2048]{0:T(1024)S(1)} %get-tuple-element.960, ...), kind=kOutput, calls=%fused_computation.29.clone.1 | convolution fusion | flops 220200960 | bytes 202756 | tf_op jit(solution)/shard_map/while/body/eval_jaxpr/dot_general | solution.py:140
  142.3 6.2 %fusion.222 = f32[8,16,512]{2,1,0:T(8,128)S(1)} fusion(f32[8,16,512]{2,1,0:T(8,128)S(1)} %get-tuple-element.939, s32[]{:T(128)S(6)} %copy.91, f32[16,2048]{1,0:T(8,128)S(1)} %get-tuple-element.963, f32[2048]{0:T(1024)S(1)} %get-tuple-element.962, f32[512]{0:T(512)S(1)} %dynamic_slice.110, f32[2048]{0:T(1024)S(1)} %get-tuple-element.960, ...), kind=kOutput, calls=%fused_computation.29.clone.1 | convolution fusion | flops 220200960 | bytes 202756 | tf_op jit(solution)/shard_map/while/body/eval_jaxpr/dot_general | solution.py:140
  150.0 6.2 %fusion.222 = f32[8,16,512]{2,1,0:T(8,128)S(1)} fusion(f32[8,16,512]{2,1,0:T(8,128)S(1)} %get-tuple-element.939, s32[]{:T(128)S(6)} %copy.91, f32[16,2048]{1,0:T(8,128)S(1)} %get-tuple-element.963, f32[2048]{0:T(1024)S(1)} %get-tuple-element.962, f32[512]{0:T(512)S(1)} %dynamic_slice.110, f32[2048]{0:T(1024)S(1)} %get-tuple-element.960, ...), kind=kOutput, calls=%fused_computation.29.clone.1 | convolution fusion | flops 220200960 | bytes 202756 | tf_op jit(solution)/shard_map/while/body/eval_jaxpr/dot_general | solution.py:140
  157.6 6.2 %fusion.222 = f32[8,16,512]{2,1,0:T(8,128)S(1)} fusion(f32[8,16,512]{2,1,0:T(8,128)S(1)} %get-tuple-element.939, s32[]{:T(128)S(6)} %copy.91, f32[16,2048]{1,0:T(8,128)S(1)} %get-tuple-element.963, f32[2048]{0:T(1024)S(1)} %get-tuple-element.962, f32[512]{0:T(512)S(1)} %dynamic_slice.110, f32[2048]{0:T(1024)S(1)} %get-tuple-element.960, ...), kind=kOutput, calls=%fused_computation.29.clone.1 | convolution fusion | flops 220200960 | bytes 202756 | tf_op jit(solution)/shard_map/while/body/eval_jaxpr/dot_general | solution.py:140
  165.3 6.2 %fusion.222 = f32[8,16,512]{2,1,0:T(8,128)S(1)} fusion(f32[8,16,512]{2,1,0:T(8,128)S(1)} %get-tuple-element.939, s32[]{:T(128)S(6)} %copy.91, f32[16,2048]{1,0:T(8,128)S(1)} %get-tuple-element.963, f32[2048]{0:T(1024)S(1)} %get-tuple-element.962, f32[512]{0:T(512)S(1)} %dynamic_slice.110, f32[2048]{0:T(1024)S(1)} %get-tuple-element.960, ...), kind=kOutput, calls=%fused_computation.29.clone.1 | convolution fusion | flops 220200960 | bytes 202756 | tf_op jit(solution)/shard_map/while/body/eval_jaxpr/dot_general | solution.py:140
  173.0 6.2 %fusion.222 = f32[8,16,512]{2,1,0:T(8,128)S(1)} fusion(f32[8,16,512]{2,1,0:T(8,128)S(1)} %get-tuple-element.939, s32[]{:T(128)S(6)} %copy.91, f32[16,2048]{1,0:T(8,128)S(1)} %get-tuple-element.963, f32[2048]{0:T(1024)S(1)} %get-tuple-element.962, f32[512]{0:T(512)S(1)} %dynamic_slice.110, f32[2048]{0:T(1024)S(1)} %get-tuple-element.960, ...), kind=kOutput, calls=%fused_computation.29.clone.1 | convolution fusion | flops 220200960 | bytes 202756 | tf_op jit(solution)/shard_map/while/body/eval_jaxpr/dot_general | solution.py:140
  179.7 10.4 %all_to_all.85 = f32[16,1,4096]{2,1,0:T(1,128)S(1)} all-to-all(f32[16,1,4096]{2,1,0:T(1,128)S(1)} %reshape.119), channel_id=1, replica_groups=mesh['sta'=16,'cel'=16] {'cel'}, dimensions={0} | all-to-all | bytes 524288 | tf_op jit(solution)/shard_map/all_to_all | solution.py:45
  195.7 7.8 %all-to-all-done.5 = f32[16,1,4096]{2,1,0:T(1,128)S(1)} async-done(((f32[16,1,4096]{2,1,0:T(1,128)}), f32[16,1,4096]{2,1,0:T(1,128)S(1)}, u32[]{:S(2)}, u32[]{:S(2)}) %all-to-all-start.5) | async-done | bytes 262176 | tf_op jit(solution)/shard_map/all_to_all | solution.py:15
  204.2 15.5 %all_to_all.81 = f32[16,1,512]{2,1,0:T(1,128)S(1)} all-to-all(f32[16,1,512]{2,1,0:T(1,128)S(1)} %reshape.125), channel_id=1, replica_groups=mesh['sta'=16,'cel'=16] {'sta'}, dimensions={0} | all-to-all | bytes 65536 | tf_op jit(solution)/shard_map/all_to_all | solution.py:15
  226.0 7.4 %all-to-all-done.7 = f32[16,1,256]{2,1,0:T(1,128)S(1)} async-done(((f32[16,1,256]{2,1,0:T(1,128)}), f32[16,1,256]{2,1,0:T(1,128)S(1)}, u32[]{:S(2)}, u32[]{:S(2)}) %all-to-all-start.7) | async-done | bytes 16416 | tf_op jit(solution)/shard_map/all_to_all | solution.py:15
  238.8 39.5 %while.51 = (s32[]{:T(128)}, f32[16,2048]{1,0:T(8,128)S(1)}, f32[16,4096]{1,0:T(8,128)S(1)}, f32[2048]{0:T(1024)S(1)}, f32[4096]{0:T(1024)S(1)}, /*index=5*/f32[...) while((s32[]{:T(128)}, f32[16,2048]{1,0:T(8,128)S(1)}, ...), condition=%wide.region_13.17_spmd.clone, body=%wide.region_12.16_spmd.clone.sunk | while | flops 220268544 | bytes 362709 | solution.py:134
  248.9 4.7 %fusion.231 = f32[16,2048]{1,0:T(8,128)S(1)} fusion(f32[2048]{0:T(1024)S(1)} %get-tuple-element.1005, f32[512]{0:T(512)S(1)} %dynamic_slice.122, f32[2048]{0:T(1024)S(1)} %get-tuple-element.1003, f32[512]{0:T(512)S(1)} %dynamic_slice.123, f32[2048]{0:T(1024)S(1)} %get-tuple-element.1001, f32[512]{0:T(512)S(1)} %dynamic_slice.124, ...), kind=kOutput, calls=%fused_computation.119.clone.1 | convolution fusion | flops 220266496 | bytes 333829 | tf_op jit(solution)/shard_map/while/body/eval_jaxpr/dot_general | solution.py:72
  253.8 4.7 %fusion.231 = f32[16,2048]{1,0:T(8,128)S(1)} fusion(f32[2048]{0:T(1024)S(1)} %get-tuple-element.1005, f32[512]{0:T(512)S(1)} %dynamic_slice.122, f32[2048]{0:T(1024)S(1)} %get-tuple-element.1003, f32[512]{0:T(512)S(1)} %dynamic_slice.123, f32[2048]{0:T(1024)S(1)} %get-tuple-element.1001, f32[512]{0:T(512)S(1)} %dynamic_slice.124, ...), kind=kOutput, calls=%fused_computation.119.clone.1 | convolution fusion | flops 220266496 | bytes 333829 | tf_op jit(solution)/shard_map/while/body/eval_jaxpr/dot_general | solution.py:72
  278.4 10.5 %all_to_all.86 = f32[16,1,2048]{2,1,0:T(1,128)S(1)} all-to-all(f32[16,1,2048]{2,1,0:T(1,128)S(1)} %reshape.115), channel_id=1, replica_groups=mesh['sta'=16,'cel'=16] {'sta'}, dimensions={0} | all-to-all | bytes 262144 | tf_op jit(solution)/shard_map/all_to_all | solution.py:45
  289.1 10.8 %all_to_all.82 = f32[16,1,2048]{2,1,0:T(1,128)S(1)} all-to-all(f32[16,1,2048]{2,1,0:T(1,128)S(1)} %broadcast_in_dim.106), channel_id=1, replica_groups=mesh['sta'=16,'cel'=16] {'sta'}, dimensions={0} | all-to-all | bytes 262144 | tf_op jit(solution)/shard_map/all_to_all | solution.py:15
  300.3 11.0 %all_to_all.83 = f32[16,1,512]{2,1,0:T(1,128)S(1)} all-to-all(f32[16,1,512]{2,1,0:T(1,128)S(1)} %reshape.129), channel_id=1, replica_groups=mesh['sta'=16,'cel'=16] {'cel'}, dimensions={0} | all-to-all | bytes 65536 | tf_op jit(solution)/shard_map/all_to_all | solution.py:15
  317.2 7.0 %all-to-all-done.11 = f32[16,1,256]{2,1,0:T(1,128)S(1)} async-done(((f32[16,1,256]{2,1,0:T(1,128)}), f32[16,1,256]{2,1,0:T(1,128)S(1)}, u32[]{:S(2)}, u32[]{:S(2)}) %all-to-all-start.11) | async-done | bytes 16416 | tf_op jit(solution)/shard_map/all_to_all | solution.py:15
  329.7 61.5 %while.49 = (s32[]{:T(128)}, f32[8,16,512]{2,1,0:T(8,128)S(1)}, f32[2048]{0:T(1024)S(1)}, s32[8]{0:T(128)S(1)}, f32[4096]{0:T(1024)S(1)}, /*index=5*/f32[2048]{0...) while((s32[]{:T(128)}, f32[8,16,512]{2,1,0:T(8,128)S(1)}, ...), condition=%wide.region_18.22_spmd, body=%wide.region_17.21_spmd.sunk | while | flops 220203008 | bytes 231647 | solution.py:148
  331.2 6.2 %fusion.225 = f32[8,16,512]{2,1,0:T(8,128)S(1)} fusion(f32[8,16,512]{2,1,0:T(8,128)S(1)} %get-tuple-element.1026, s32[]{:T(128)S(6)} %copy.103, f32[16,2048]{1,0:T(8,128)S(1)} %get-tuple-element.1050, f32[2048]{0:T(1024)S(1)} %get-tuple-element.1049, f32[512]{0:T(512)S(1)} %dynamic_slice.114, f32[2048]{0:T(1024)S(1)} %get-tuple-element.1047, ...), kind=kOutput, calls=%fused_computation.62.clone.1 | convolution fusion | flops 220200960 | bytes 202756 | tf_op jit(solution)/shard_map/while/body/eval_jaxpr/dot_general | solution.py:140
  338.8 6.2 %fusion.225 = f32[8,16,512]{2,1,0:T(8,128)S(1)} fusion(f32[8,16,512]{2,1,0:T(8,128)S(1)} %get-tuple-element.1026, s32[]{:T(128)S(6)} %copy.103, f32[16,2048]{1,0:T(8,128)S(1)} %get-tuple-element.1050, f32[2048]{0:T(1024)S(1)} %get-tuple-element.1049, f32[512]{0:T(512)S(1)} %dynamic_slice.114, f32[2048]{0:T(1024)S(1)} %get-tuple-element.1047, ...), kind=kOutput, calls=%fused_computation.62.clone.1 | convolution fusion | flops 220200960 | bytes 202756 | tf_op jit(solution)/shard_map/while/body/eval_jaxpr/dot_general | solution.py:140
  346.5 6.2 %fusion.225 = f32[8,16,512]{2,1,0:T(8,128)S(1)} fusion(f32[8,16,512]{2,1,0:T(8,128)S(1)} %get-tuple-element.1026, s32[]{:T(128)S(6)} %copy.103, f32[16,2048]{1,0:T(8,128)S(1)} %get-tuple-element.1050, f32[2048]{0:T(1024)S(1)} %get-tuple-element.1049, f32[512]{0:T(512)S(1)} %dynamic_slice.114, f32[2048]{0:T(1024)S(1)} %get-tuple-element.1047, ...), kind=kOutput, calls=%fused_computation.62.clone.1 | convolution fusion | flops 220200960 | bytes 202756 | tf_op jit(solution)/shard_map/while/body/eval_jaxpr/dot_general | solution.py:140
  354.2 6.2 %fusion.225 = f32[8,16,512]{2,1,0:T(8,128)S(1)} fusion(f32[8,16,512]{2,1,0:T(8,128)S(1)} %get-tuple-element.1026, s32[]{:T(128)S(6)} %copy.103, f32[16,2048]{1,0:T(8,128)S(1)} %get-tuple-element.1050, f32[2048]{0:T(1024)S(1)} %get-tuple-element.1049, f32[512]{0:T(512)S(1)} %dynamic_slice.114, f32[2048]{0:T(1024)S(1)} %get-tuple-element.1047, ...), kind=kOutput, calls=%fused_computation.62.clone.1 | convolution fusion | flops 220200960 | bytes 202756 | tf_op jit(solution)/shard_map/while/body/eval_jaxpr/dot_general | solution.py:140
  361.9 6.2 %fusion.225 = f32[8,16,512]{2,1,0:T(8,128)S(1)} fusion(f32[8,16,512]{2,1,0:T(8,128)S(1)} %get-tuple-element.1026, s32[]{:T(128)S(6)} %copy.103, f32[16,2048]{1,0:T(8,128)S(1)} %get-tuple-element.1050, f32[2048]{0:T(1024)S(1)} %get-tuple-element.1049, f32[512]{0:T(512)S(1)} %dynamic_slice.114, f32[2048]{0:T(1024)S(1)} %get-tuple-element.1047, ...), kind=kOutput, calls=%fused_computation.62.clone.1 | convolution fusion | flops 220200960 | bytes 202756 | tf_op jit(solution)/shard_map/while/body/eval_jaxpr/dot_general | solution.py:140
  369.6 6.2 %fusion.225 = f32[8,16,512]{2,1,0:T(8,128)S(1)} fusion(f32[8,16,512]{2,1,0:T(8,128)S(1)} %get-tuple-element.1026, s32[]{:T(128)S(6)} %copy.103, f32[16,2048]{1,0:T(8,128)S(1)} %get-tuple-element.1050, f32[2048]{0:T(1024)S(1)} %get-tuple-element.1049, f32[512]{0:T(512)S(1)} %dynamic_slice.114, f32[2048]{0:T(1024)S(1)} %get-tuple-element.1047, ...), kind=kOutput, calls=%fused_computation.62.clone.1 | convolution fusion | flops 220200960 | bytes 202756 | tf_op jit(solution)/shard_map/while/body/eval_jaxpr/dot_general | solution.py:140
  377.3 6.2 %fusion.225 = f32[8,16,512]{2,1,0:T(8,128)S(1)} fusion(f32[8,16,512]{2,1,0:T(8,128)S(1)} %get-tuple-element.1026, s32[]{:T(128)S(6)} %copy.103, f32[16,2048]{1,0:T(8,128)S(1)} %get-tuple-element.1050, f32[2048]{0:T(1024)S(1)} %get-tuple-element.1049, f32[512]{0:T(512)S(1)} %dynamic_slice.114, f32[2048]{0:T(1024)S(1)} %get-tuple-element.1047, ...), kind=kOutput, calls=%fused_computation.62.clone.1 | convolution fusion | flops 220200960 | bytes 202756 | tf_op jit(solution)/shard_map/while/body/eval_jaxpr/dot_general | solution.py:140
  385.0 6.2 %fusion.225 = f32[8,16,512]{2,1,0:T(8,128)S(1)} fusion(f32[8,16,512]{2,1,0:T(8,128)S(1)} %get-tuple-element.1026, s32[]{:T(128)S(6)} %copy.103, f32[16,2048]{1,0:T(8,128)S(1)} %get-tuple-element.1050, f32[2048]{0:T(1024)S(1)} %get-tuple-element.1049, f32[512]{0:T(512)S(1)} %dynamic_slice.114, f32[2048]{0:T(1024)S(1)} %get-tuple-element.1047, ...), kind=kOutput, calls=%fused_computation.62.clone.1 | convolution fusion | flops 220200960 | bytes 202756 | tf_op jit(solution)/shard_map/while/body/eval_jaxpr/dot_general | solution.py:140
  391.7 10.4 %all_to_all.87 = f32[16,1,4096]{2,1,0:T(1,128)S(1)} all-to-all(f32[16,1,4096]{2,1,0:T(1,128)S(1)} %reshape.120), channel_id=1, replica_groups=mesh['sta'=16,'cel'=16] {'cel'}, dimensions={0} | all-to-all | bytes 524288 | tf_op jit(solution)/shard_map/all_to_all | solution.py:45
  402.4 12.0 %all_to_all.88 = f32[16,1,4096]{2,1,0:T(1,128)S(1)} all-to-all(f32[16,1,4096]{2,1,0:T(1,128)S(1)} %broadcast_in_dim.109), channel_id=1, replica_groups=mesh['sta'=16,'cel'=16] {'cel'}, dimensions={0} | all-to-all | bytes 524288 | tf_op jit(solution)/shard_map/all_to_all | solution.py:15
  416.0 8.7 %all-to-all-start.14 = ((f32[16,1,768]{2,1,0:T(1,128)}), f32[16,1,768]{2,1,0:T(1,128)S(1)}, u32[]{:S(2)}, u32[]{:S(2)}) async-start(f32[16,1,768]{2,1,0:T(1,128)} %reshape.133), calls=%async_computation.14 | async-start | bytes 98304 | tf_op jit(solution)/shard_map/all_to_all | solution.py:15
  425.4 6.7 %all-to-all-done.14 = f32[16,1,768]{2,1,0:T(1,128)S(1)} async-done(((f32[16,1,768]{2,1,0:T(1,128)}), f32[16,1,768]{2,1,0:T(1,128)S(1)}, u32[]{:S(2)}, u32[]{:S(2)}) %all-to-all-start.14) | async-done | bytes 49184 | tf_op jit(solution)/shard_map/all_to_all | solution.py:15
  439.1 6.8 %all-to-all-done.15 = f32[16,1,256]{2,1,0:T(1,128)S(1)} async-done(((f32[16,1,256]{2,1,0:T(1,128)}), f32[16,1,256]{2,1,0:T(1,128)S(1)}, u32[]{:S(2)}, u32[]{:S(2)}) %all-to-all-start.15) | async-done | bytes 16416 | tf_op jit(solution)/shard_map/all_to_all | solution.py:15
  (287 shorter events, 114.5 us)
Async XLA Ops:
  54.8 27.7 %copy-start.3 = (f32[16,2048]{1,0:T(8,128)S(1)}, f32[16,2048]{1,0:T(8,128)}, u32[]{:S(2)}) copy-start(f32[16,2048]{1,0:T(8,128)} %param.28) | copy-start | bytes 393220
  55.6 16.1 %all-to-all-start = ((f32[16,1,2048]{2,1,0:T(1,128)}), f32[16,1,2048]{2,1,0:T(1,128)S(1)}, u32[]{:S(2)}, u32[]{:S(2)}) async-start(f32[16,1,2048]{2,1,0:T(1,128)} %reshape.111), calls=%async_computation | async-start | bytes 262144 | tf_op jit(solution)/shard_map/all_to_all | solution.py:45
  101.4 16.3 %copy-start = (f32[2048]{0:T(1024)S(1)}, f32[2048]{0:T(1024)}, u32[]{:S(2)}) copy-start(f32[2048]{0:T(1024)} %get-tuple-element.1055) | copy-start | bytes 24580
  101.4 10.9 %all-to-all-start.3 = ((f32[16,1,256]{2,1,0:T(1,128)}), f32[16,1,256]{2,1,0:T(1,128)S(1)}, u32[]{:S(2)}, u32[]{:S(2)}) async-start(f32[16,1,256]{2,1,0:T(1,128)} %reshape.123), calls=%async_computation.3 | async-start | bytes 32768 | tf_op jit(solution)/shard_map/all_to_all | solution.py:15
  190.1 5.5 %copy-start.2 = (f32[16,4096]{1,0:T(8,128)S(1)}, f32[16,4096]{1,0:T(8,128)}, u32[]{:S(2)}) copy-start(f32[16,4096]{1,0:T(8,128)} %param.26) | copy-start | bytes 786436
  191.1 4.5 copy-start.1
  191.1 12.3 %all-to-all-start.5 = ((f32[16,1,4096]{2,1,0:T(1,128)}), f32[16,1,4096]{2,1,0:T(1,128)S(1)}, u32[]{:S(2)}, u32[]{:S(2)}) async-start(f32[16,1,4096]{2,1,0:T(1,128)} %broadcast_in_dim.103), calls=%async_computation.5 | async-start | bytes 524288 | tf_op jit(solution)/shard_map/all_to_all | solution.py:15
  222.3 11.0 %all-to-all-start.7 = ((f32[16,1,256]{2,1,0:T(1,128)}), f32[16,1,256]{2,1,0:T(1,128)S(1)}, u32[]{:S(2)}, u32[]{:S(2)}) async-start(f32[16,1,256]{2,1,0:T(1,128)} %reshape.127), calls=%async_computation.7 | async-start | bytes 32768 | tf_op jit(solution)/shard_map/all_to_all | solution.py:15
  313.5 10.8 %all-to-all-start.11 = ((f32[16,1,256]{2,1,0:T(1,128)}), f32[16,1,256]{2,1,0:T(1,128)S(1)}, u32[]{:S(2)}, u32[]{:S(2)}) async-start(f32[16,1,256]{2,1,0:T(1,128)} %reshape.131), calls=%async_computation.11 | async-start | bytes 32768 | tf_op jit(solution)/shard_map/all_to_all | solution.py:15
  416.0 16.1 %all-to-all-start.14 = ((f32[16,1,768]{2,1,0:T(1,128)}), f32[16,1,768]{2,1,0:T(1,128)S(1)}, u32[]{:S(2)}, u32[]{:S(2)}) async-start(f32[16,1,768]{2,1,0:T(1,128)} %reshape.133), calls=%async_computation.14 | async-start | bytes 98304 | tf_op jit(solution)/shard_map/all_to_all | solution.py:15
  434.8 11.0 %all-to-all-start.15 = ((f32[16,1,256]{2,1,0:T(1,128)}), f32[16,1,256]{2,1,0:T(1,128)S(1)}, u32[]{:S(2)}, u32[]{:S(2)}) async-start(f32[16,1,256]{2,1,0:T(1,128)} %reshape.135), calls=%async_computation.15 | async-start | bytes 32768 | tf_op jit(solution)/shard_map/all_to_all | solution.py:15
where the time goes:
time: 455 us; the launch traced here: 453 us
  matrix products  187 us (41%)
  blocking collectives  107 us (24%)
  waiting for transfers between devices  50.3 us (11%)
  starting transfers between devices  36.5 us (8%)
  other arithmetic  33.5 us (7%)
  local copies, waits for them, and re-layouts  26.4 us (6%)
  loops' own time  10.7 us (2%)
    dot_general x16, matrix products, one_block(): lax.dot_general(right, tile_at(index * block), (((1,), (1,)), ((), ())),...  99 us
    dot_general x28, matrix products, matmul(): return jnp.dot(a, b, precision=HIGH, preferred_element_type=jnp.float32)  86.1 us
    all_to_all x6, blocking collectives, sent_to_all(): return lax.all_to_all(copies, axis, split_axis=0, concat_axis=0, tiled=True)  75.4 us
    all_to_all x6, waiting for transfers between devices, sent_to_all(): return lax.all_to_all(copies, axis, split_axis=0, concat_axis=0, tiled=True)  42.7 us
    all_to_all x3, blocking collectives, sent_and_summed(): lax.all_to_all(cut_along(value, dim, length), axis, 0, 0, tiled=True)  31.2 us
    all_to_all x6, starting transfers between devices, sent_to_all(): return lax.all_to_all(copies, axis, split_axis=0, concat_axis=0, tiled=True)  28.1 us
    another operation x2, loops' own time, body(): parts = lax.map(one_block, jnp.arange(count))  10.6 us
    dynamic_slice x16, local copies, waits for them, and re-layouts, body(): parts = lax.map(one_block, jnp.arange(count))  9.59 us
  transfers between devices with their start and end apart: 7, of which 7 were waited for; matrix products, arithmetic and copies ran while one was open for 0% of the time, Pallas kernels for 0%

commit v1 on v0

v1 whole, which is shorter than its diff:
```python
import functools

import jax
import jax.numpy as jnp
from jax import lax
from jax.experimental import pallas as pl
from jax.experimental.pallas import tpu as pltpu
from jax.sharding import PartitionSpec as P

F32 = jnp.float32
BF16 = jnp.bfloat16
HIGH = lax.Precision.HIGHEST
TILE = 256
NN = (((1,), (0,)), ((), ()))
NT = (((1,), (1,)), ((), ()))


def fdot(a, b, dims=NN):
    return lax.dot_general(a, b, dims, precision=HIGH, preferred_element_type=F32)


def bdot(a, b, dims=NN):
    return lax.dot_general(a, b, dims, preferred_element_type=F32)


def halves(x):
    hi = x.astype(BF16)
    lo = (x - hi.astype(F32)).astype(BF16)
    return hi, lo


def lanes(blocks, width):
    used = sum(b.shape[1] for b in blocks)
    rows = blocks[0].shape[0]
    return jnp.concatenate([*blocks, jnp.zeros((rows, width - used), F32)], axis=1)


def block_of(stats, index):
    return stats[:, 16 * index : 16 * index + 16]


def wide(stats):
    return jnp.concatenate([stats[:8], stats[8:]], axis=1)


def tall(stats):
    return jnp.concatenate([stats[:, :128], stats[:, 128:]], axis=0)


def factor(gram):
    size = gram.shape[0]
    row = lax.broadcasted_iota(jnp.int32, (size, 1), 0)
    lane = lax.broadcasted_iota(jnp.int32, (size, size), 1)
    eye = jnp.where(lax.broadcasted_iota(jnp.int32, (size, size), 0) == lane, 1.0, 0.0)
    work, inv = gram, eye
    lower = jnp.zeros_like(gram)
    for k in range(size):
        pivot = work[k : k + 1, k : k + 1]
        r = lax.rsqrt(pivot)
        r = r * (1.5 - 0.5 * pivot * r * r)
        col = work[:, k : k + 1] * r
        lower = jnp.where((lane == k) & (row >= k), col, lower)
        below = jnp.where(row > k, col, 0.0)
        work_row = work[k : k + 1, :] * r
        inv_row = inv[k : k + 1, :] * r
        work = work - below * work_row
        inv = jnp.where(row == k, inv_row, inv - below * inv_row)
    return lower, inv


def orthonormal(onto, basis, own):
    count = len(onto)
    gram = own
    for l in range(count):
        part = -2.0 * onto[l]
        for m in range(count):
            if m >= l:
                part = part + fdot(onto[m], basis[m][l])
            else:
                part = part + fdot(onto[m], basis[l][m], NT)
        gram = gram + fdot(part, onto[l], NT)
    lower, inv = factor(gram)
    return lower, jnp.concatenate([inv] + [-fdot(inv, c) for c in onto], axis=1)


def added(ref):
    total = ref[0]
    for k in range(1, ref.shape[0]):
        total = total + ref[k]
    return total


def copies(ref, value):
    for k in range(ref.shape[0]):
        ref[k] = value


def gathered(ref):
    return jnp.concatenate([ref[k] for k in range(ref.shape[0])], axis=1)


def stack_of(*values):
    parts = [halves(v) for v in values]
    return jnp.concatenate([p[0] for p in parts] + [p[1] for p in parts], axis=0)


def products(x, y):
    m, k = x.shape[0] // 2, y.shape[0] // 2
    full = bdot(x, y, NT)
    return full[:m, :k] + (full[:m, k:] + full[m:, :k]) + full[m:, k:]


PARTS = 2


def first_pass(sp, sh, cp, cd, rho, lb, ln, *refs):
    matrix, (out, rows, st, ce, cxb, cyb, czb) = refs[: 2 * PARTS], refs[2 * PARTS :]
    n_s, n_c = st.shape[1], ce.shape[1]
    st[0:2, :] = sp[...].astype(F32)
    st[2:3, :] = sh[...].astype(F32) + 0.5
    ce[...] = jnp.zeros_like(ce)
    ce[0:2, :] = cp[...].astype(F32)
    ce[2:3, :] = cd[...].astype(F32)
    rows[...] = stack_of(ln[...], lb[...])
    gram = products(rows[...], rows[...])
    stats = lanes([gram[16:, 16:], gram[:16, 16:], gram[:16, :16]], 128)

    def both(ref, r0):
        return jnp.concatenate([ref[r0 : r0 + 8, :]] * 2, axis=1)

    def cell_block(part, cb, carry):
        hi_ref, lo_ref = matrix[2 * part], matrix[2 * part + 1]
        g0 = pl.multiple_of(cb * TILE, TILE)
        c0 = part * (n_c // PARTS) + g0
        for half in range(2):
            turned = jnp.transpose(ce[:, pl.ds(pl.multiple_of(c0 + 128 * half, 128), 128)])
            put = slice(128 * half, 128 * half + 128)
            cxb[put, :] = jnp.broadcast_to(turned[:, 0:1], (128, 128))
            cyb[put, :] = jnp.broadcast_to(turned[:, 1:2], (128, 128))
            czb[put, :] = jnp.broadcast_to(turned[:, 2:3], (128, 128))

        def station_block(sb, inner):
            here = pl.ds(pl.multiple_of(sb * TILE, TILE), TILE)
            sx = jnp.broadcast_to(st[0:1, here], (8, TILE))
            sy = jnp.broadcast_to(st[1:2, here], (8, TILE))
            sz = jnp.broadcast_to(st[2:3, here], (8, TILE))
            for r0 in range(0, TILE, 8):
                dx = sx - both(cxb, r0)
                dy = sy - both(cyb, r0)
                dz = sz + both(czb, r0)
                dz2 = dz * dz
                inv = lax.rsqrt(dx * dx + dy * dy + dz2)
                inv2 = inv * inv
                g = (dz2 * inv2 - (1.0 / 3.0)) * (inv2 * inv)
                g_hi = g.astype(BF16)
                where = pl.ds(pl.multiple_of(g0 + r0, 8), 8)
                hi_ref[where, here] = g_hi
                lo_ref[where, here] = (g - g_hi.astype(F32)).astype(BF16)
            return inner

        lax.fori_loop(0, n_s // TILE, station_block, 0)
        big = bdot(rows[...], hi_ref[pl.ds(g0, TILE), :], NT)
        small = bdot(rows[:32, :], lo_ref[pl.ds(g0, TILE), :], NT)
        total = (big[:32] + big[32:] + small) * (12.0 * rho[0:1, pl.ds(pl.multiple_of(c0, TILE), TILE)])
        for k in range(2):
            piece = 2 * cb + k + part * (n_c // PARTS // 128)
            out[piece, :32, :] = total[:, 128 * k : 128 * k + 128]
            out[piece, 32:, :] = stats
        return carry

    for part in range(PARTS):
        lax.fori_loop(0, n_c // PARTS // TILE, functools.partial(cell_block, part), 0)


def first_sum(rs, ag, keep):
    total = added(rs)
    keep[...] = total
    copies(ag, total[:16])


def forward_product(rows, count, matrix, out, stats):
    step = 2 * TILE
    size = matrix[0].shape[0]

    def station_block(sb, carry):
        s0 = pl.multiple_of(sb * step, step)
        total = jnp.zeros((count, step), F32)
        for part in range(PARTS):
            own = slice(part * size, part * size + size)
            big = bdot(rows[:, own], matrix[2 * part][:, pl.ds(s0, step)])
            small = bdot(rows[:count, own], matrix[2 * part + 1][:, pl.ds(s0, step)])
            total = total + (big[:count] + big[count:] + small)
        for k in range(2):
            out[2 * sb + k, :count, :] = total[:, TILE * k : TILE * k + TILE]
            out[2 * sb + k, count:, :] = stats
        return carry

    lax.fori_loop(0, matrix[0].shape[1] // step, station_block, 0)


def second_pass(ag, q, rho, *refs):
    matrix, (out, rows) = refs[: 2 * PARTS], refs[2 * PARTS :]
    w = gathered(ag)
    base = q[...]
    scale = 12.0 * rho[...]
    rows[...] = stack_of(w * scale, base * scale)
    pair = stack_of(w, base)
    gram = products(pair, pair)
    stats = lanes([gram[16:, 16:], gram[:16, 16:], gram[:16, :16]], 128)
    forward_product(rows, 32, matrix, out, wide(stats))


def second_sum(cells, rs, ag, keep, stats_out, t_out, l_out):
    total = added(rs)
    stats = tall(total[32:]) * (1.0 / cells)
    stats_out[...] = stats
    lower, t = orthonormal([block_of(stats, 1)], [[block_of(stats, 0)]], block_of(stats, 2))
    l_out[...] = lower
    t_out[...] = t
    v = fdot(t, total[:32])
    keep[...] = jnp.concatenate([v, total[16:32]], axis=0)
    copies(ag, v)


def third_pass(ag, left_rows, rho, *refs):
    matrix, (out, rows) = refs[: 2 * PARTS], refs[2 * PARTS :]
    v = gathered(ag)
    rows[...] = stack_of(v)
    gram = products(rows[...], left_rows[...])
    stats = lanes([gram[:, 16:], gram[:, :16], products(rows[...], rows[...])], 128)

    size = matrix[0].shape[0]

    def cell_block(part, cb, carry):
        g0 = pl.multiple_of(cb * TILE, TILE)
        c0 = pl.multiple_of(part * size + g0, TILE)
        big = bdot(rows[...], matrix[2 * part][pl.ds(g0, TILE), :], NT)
        small = bdot(rows[:16, :], matrix[2 * part + 1][pl.ds(g0, TILE), :], NT)
        total = (big[:16] + big[16:] + small) * (12.0 * rho[0:1, pl.ds(c0, TILE)])
        for k in range(2):
            piece = 2 * cb + k + part * (size // 128)
            out[piece, :16, :] = total[:, 128 * k : 128 * k + 128]
            out[piece, 16:, :] = stats
        return carry

    for part in range(PARTS):
        lax.fori_loop(0, size // TILE, functools.partial(cell_block, part), 0)


def third_sum(stations, rs, keep0, ag, t_out, l_out):
    total = added(rs)
    stats = total[16:] * (1.0 / stations)
    base = keep0[32:48, :] * (1.0 / stations)
    grams = [[block_of(base, 0)], [block_of(base, 1), block_of(base, 2)]]
    lower, t = orthonormal([block_of(stats, 0), block_of(stats, 1)], grams, block_of(stats, 2))
    l_out[...] = lower
    t_out[...] = t
    w = fdot(t, jnp.concatenate([total[:16], keep0[16:32, :], keep0[:16, :]], axis=0))
    copies(ag, w)


def fourth_pass(ag2, ag0, q, rho, t1, *refs):
    matrix, (right_out, out, rows) = refs[: 2 * PARTS], refs[2 * PARTS :]
    base = q[...]
    right = fdot(t1[...], jnp.concatenate([gathered(ag0), base], axis=0))
    right_out[...] = right
    w = gathered(ag2)
    rows[...] = stack_of(w * (12.0 * rho[...]))
    gram = products(stack_of(right, w), stack_of(base, right, w))
    stats = lanes([gram[:16, :32], gram[16:, :48]], 128)
    forward_product(rows, 16, matrix, out, wide(stats))


def fourth_sum(cells, rs, keep1, stats1, ag, t_out, l_out):
    total = added(rs)
    stats = tall(total[16:]) * (1.0 / cells)
    grams = [[block_of(stats1[...], 0)], [block_of(stats, 0), block_of(stats, 1)]]
    lower, t = orthonormal([block_of(stats, 2), block_of(stats, 3)], grams, block_of(stats, 4))
    l_out[...] = lower
    t_out[...] = t
    v = fdot(t, jnp.concatenate([total[:16], keep1[16:, :], keep1[:16, :]], axis=0))
    copies(ag, v)


def last_stats(ag3, ag1, lb, ln, t2, left_out, out):
    before, now = lb[...], ln[...]
    left = fdot(t2[...], jnp.concatenate([gathered(ag1), before, now], axis=0))
    left_out[...] = left
    v = gathered(ag3)
    gram = products(stack_of(left, v), stack_of(before, now, left, v))
    copies(out, lanes([gram[:16, :48], gram[16:, :64]], 128))


def finish(stations, rs, keep0, ag3, lb, ln, left1, ag2, q, right1, t3, l1, l2, l3, rights, left_out, alphas, betas):
    stats = added(rs) * (1.0 / stations)
    base = keep0[32:48, :] * (1.0 / stations)
    grams = [
        [block_of(base, 0)],
        [block_of(base, 1), block_of(base, 2)],
        [block_of(stats, 0), block_of(stats, 1), block_of(stats, 2)],
    ]
    onto = [block_of(stats, 3), block_of(stats, 4), block_of(stats, 5)]
    lower, t = orthonormal(onto, grams, block_of(stats, 6))
    left_out[...] = fdot(t, jnp.concatenate([gathered(ag3), lb[...], ln[...], left1[...]], axis=0))
    rights[0] = right1[...]
    rights[1] = fdot(t3[...], jnp.concatenate([gathered(ag2), q[...], right1[...]], axis=0))
    alphas[0] = l1[...]
    alphas[1] = l3[...]
    betas[0] = l2[...]
    betas[1] = lower


def call(kernel, args, outs, scratch=(), limit=4):
    spec = pl.BlockSpec(memory_space=pltpu.VMEM)
    return pl.pallas_call(
        kernel,
        out_shape=tuple(outs),
        in_specs=[spec] * len(args),
        out_specs=tuple(spec for _ in outs),
        scratch_shapes=list(scratch),
        compiler_params=pltpu.CompilerParams(vmem_limit_bytes=limit * 2**20),
    )(*args)


def f32(*shape):
    return jax.ShapeDtypeStruct(shape, F32)


def exchange(value, axis):
    return lax.all_to_all(value, axis, split_axis=0, concat_axis=0, tiled=True)


def body(station_plane, station_height, cell_plane, cell_depth, cell_density, left_before, left_now, right_before):
    n_s, n_c = left_now.shape[1], right_before.shape[1]
    n_sta, n_cel = lax.axis_size("sta"), lax.axis_size("cel")
    stations, cells = n_s * n_sta, n_c * n_cel
    cp, sp = n_c // n_sta, n_s // n_cel
    lb, ln, q = left_before, left_now, right_before
    rho = cell_density.reshape(1, n_c)
    small = f32(16, 16)

    *matrix, rs0, left_rows = call(
        first_pass,
        (
            station_plane,
            station_height.reshape(1, n_s),
            cell_plane,
            cell_depth.reshape(1, n_c),
            rho,
            lb,
            ln,
        ),
        (
            *[pltpu.VMEM((n_c // PARTS, n_s), BF16)] * (2 * PARTS),
            f32(n_sta, 48, cp),
            pltpu.VMEM((64, n_s), BF16),
        ),
        [
            pltpu.VMEM((8, n_s), F32),
            pltpu.VMEM((8, n_c), F32),
            pltpu.VMEM((TILE, 128), F32),
            pltpu.VMEM((TILE, 128), F32),
            pltpu.VMEM((TILE, 128), F32),
        ],
    )
    ag0, keep0 = call(first_sum, (exchange(rs0, "sta"),), (f32(n_sta, 16, cp), f32(48, cp)))
    ag0 = exchange(ag0, "sta")
    (rs1,) = call(second_pass, (ag0, q, rho, *matrix), (f32(n_cel, 40, sp),), [pltpu.VMEM((64, n_c), BF16)])
    ag1, keep1, stats1, t1, l1 = call(
        lambda *refs: second_sum(cells, *refs),
        (exchange(rs1, "cel"),),
        (f32(n_cel, 16, sp), f32(32, sp), f32(16, 128), f32(16, 32), small),
    )
    ag1 = exchange(ag1, "cel")
    (rs2,) = call(third_pass, (ag1, left_rows, rho, *matrix), (f32(n_sta, 32, cp),), [pltpu.VMEM((32, n_s), BF16)])
    ag2, t2, l2 = call(
        lambda *refs: third_sum(stations, *refs),
        (exchange(rs2, "sta"), keep0),
        (f32(n_sta, 16, cp), f32(16, 48), small),
    )
    ag2 = exchange(ag2, "sta")
    right1, rs3 = call(
        fourth_pass,
        (ag2, ag0, q, rho, t1, *matrix),
        (f32(16, n_c), f32(n_cel, 24, sp)),
        [pltpu.VMEM((32, n_c), BF16)],
    )
    ag3, t3, l3 = call(
        lambda *refs: fourth_sum(cells, *refs),
        (exchange(rs3, "cel"), keep1, stats1),
        (f32(n_cel, 16, sp), f32(16, 48), small),
    )
    ag3 = exchange(ag3, "cel")
    left1, rs4 = call(last_stats, (ag3, ag1, lb, ln, t2), (f32(16, n_s), f32(n_sta, 16, 128)))
    rights, left2, alphas, betas = call(
        lambda *refs: finish(stations, *refs),
        (exchange(rs4, "sta"), keep0, ag3, lb, ln, left1, ag2, q, right1, t3, l1, l2, l3),
        (f32(2, 16, n_c), f32(16, n_s), f32(2, 16, 16), f32(2, 16, 16)),
    )
    return rights, left2, alphas, betas


def solution(mesh):
    in_specs = (
        P(None, "sta"),
        P("sta"),
        P(None, "cel"),
        P("cel"),
        P("cel"),
        P(None, "sta"),
        P(None, "sta"),
        P(None, "cel"),
    )
    out_specs = (P(None, None, "cel"), P(None, "sta"), P(), P())
    return jax.shard_map(body, mesh=mesh, in_specs=in_specs, out_specs=out_specs, check_vma=False)
```

time: 455 us -> 217 us (0.48)
  matrix products: 187 us -> 0 us
  Pallas kernels: 0 us -> 71.8 us
  waiting for transfers between devices: 50.3 us -> 0 us
  starting transfers between devices: 36.5 us -> 0 us
  other arithmetic: 33.5 us -> 0 us
  blocking collectives: 107 us -> 136 us
  local copies, waits for them, and re-layouts: 26.4 us -> 7.09 us
  loops' own time: 10.7 us -> 0 us
    dot_general x44 -> x0, matrix products: 185 us -> none  [the longest x16 99 us: one_block(): lax.dot_general(right, tile_at(index * block), (((1,), (1,)), ((), ())),...]
    pallas_call x0 -> x10, Pallas kernels: none -> 71.8 us  [call(): pl.pallas_call(kernel, out_shape=tuple(outs), in_specs=[spec] * len(args)...]
    all_to_all x7 -> x0, waiting for transfers between devices: 50.3 us -> none  [the longest x6 42.7 us: sent_to_all(): return lax.all_to_all(copies, axis, split_axis=0, concat_axis=0, tiled=True)]
    all_to_all x7 -> x0, starting transfers between devices: 36.5 us -> none  [the longest x6 28.1 us: sent_to_all(): return lax.all_to_all(copies, axis, split_axis=0, concat_axis=0, tiled=True)]
    all_to_all x9, blocking collectives: 107 us -> 136 us  [exchange(): return lax.all_to_all(value, axis, split_axis=0, concat_axis=0, tiled=True)]
    another operation x23 -> x0, other arithmetic: 18 us -> none  [the longest x12 8.53 us: orthonormal(): lower = jnp.linalg.cholesky(gram)]
    dynamic_slice x112 -> x0, local copies, waits for them, and re-layouts: 16.8 us -> none  [the longest x16 9.59 us: body(): parts = lax.map(one_block, jnp.arange(count))]
    another operation x4 -> x0, loops' own time: 10.7 us -> none  [the longest x2 10.6 us: body(): parts = lax.map(one_block, jnp.arange(count))]
  transfers between devices with their start and end apart: 7 -> 0, of which waited for: 7 -> 0; matrix products, arithmetic and copies ran while one was open for 0% -> 0% of each run, Pallas kernels for 0% -> 0%
where the time goes in v1:
time: 217 us; the launch traced here: 216 us
  blocking collectives  136 us (63%)
  Pallas kernels  71.8 us (33%)
  local copies, waits for them, and re-layouts  7.09 us (3%)
    all_to_all x9, blocking collectives, exchange(): return lax.all_to_all(value, axis, split_axis=0, concat_axis=0, tiled=True)  136 us
    pallas_call x10, Pallas kernels, call(): pl.pallas_call(kernel, out_shape=tuple(outs), in_specs=[spec] * len(args)...  71.8 us
    unnamed x26, local copies, waits for them, and re-layouts  7.09 us

profile of v1, /device:TPU:1, one launch (start us, length us, event | category | flops | bytes accessed | tf_op | source)
XLA Modules:
  0.0 215.9 jit_solution(4180421318862061397)
XLA Ops:
  0.6 0.0 copy-start
  0.6 0.9 copy-done
  1.6 0.0 copy-start.2
  1.6 0.9 copy-done.2
  2.5 0.0 copy-start.6
  2.5 0.7 copy-done.6
  3.2 0.0 copy-start.9
  3.2 0.8 copy-done.9
  4.0 0.0 copy-start.10
  4.0 0.7 copy-done.10
  4.7 0.0 copy-start.11
  4.7 0.7 copy-done.11
  5.4 0.0 copy-start.12
  5.4 0.7 copy-done.12
  6.1 35.3 %shard_map.111 = (bf16[1024,4096]{1,0:T(8,128)(2,1)S(1)}, bf16[1024,4096]{1,0:T(8,128)(2,1)S(1)}, bf16[1024,4096]{1,0:T(8,128)(2,1)S(1)}, bf16[1024,4096]{1,0:T(...) custom-call(s32[2,4096]{1,0:T(2,128)S(1)} %copy-done.9, s32[1,4096]{1,0:T(1,128)S(1)} %bitcast.7, ...), custom_call_target="tpu_custom_call" | custom-call | tf_op jit(solution)/shard_map/pallas_call | solution.py:315
  41.4 18.0 %all_to_all.45.rs = f32[16,48,128]{2,1,0:T(8,128)S(1)} all-to-all(f32[16,48,128]{2,1,0:T(8,128)S(1)} %get-tuple-element.27), channel_id=1, replica_groups=mesh['sta'=16,'cel'=16] {'sta'}, dimensions={0} | all-to-all | bytes 786432 | tf_op jit(solution)/shard_map/all_to_all | solution.py:330
  59.4 11.4 %all_to_all.46.ag.ag0 = f32[16,16,128]{2,1,0:T(8,128)S(1)} all-to-all(f32[16,16,128]{2,1,0:T(8,128)S(1)} %get-tuple-element.28), channel_id=1, replica_groups=mesh['sta'=16,'cel'=16] {'sta'}, dimensions={0} | all-to-all | bytes 262144 | tf_op jit(solution)/shard_map/all_to_all | solution.py:330
  70.8 0.0 copy-start.4
  70.8 0.9 copy-done.4
  71.7 0.0 copy-start.7
  71.7 0.7 copy-done.7
  72.4 0.0 copy-start.8
  72.4 7.2 %shard_map.113 = f32[16,40,256]{2,1,0:T(8,128)S(1)} custom-call(f32[16,16,128]{2,1,0:T(8,128)S(1)} %all_to_all.46.ag.ag0, f32[16,2048]{1,0:T(8,128)S(1)} %copy-done.4, f32[1,2048]{1,0:T(1,128)S(1)} %bitcast.4, bf16[1024,4096]{1,0:T(8,128)(2,1)S(1)} %get-tuple-element.29.refs_0_, bf16[1024,4096]{1,0:T(8,128)(2,1)S(1)} %get-tuple-element.30.refs_1_, ...), custom_call_target="tpu_custom_call" | custom-call | tf_op jit(solution)/shard_map/pallas_call | solution.py:315
  79.6 25.5 %all_to_all.47.refs_0_ = f32[16,40,256]{2,1,0:T(8,128)S(1)} all-to-all(f32[16,40,256]{2,1,0:T(8,128)S(1)} %shard_map.113), channel_id=1, replica_groups=mesh['sta'=16,'cel'=16] {'cel'}, dimensions={0} | all-to-all | bytes 1310720 | tf_op jit(solution)/shard_map/all_to_all | solution.py:330
  105.1 2.3 %shard_map.114 = (f32[16,16,256]{2,1,0:T(8,128)S(1)}, f32[32,256]{1,0:T(8,128)S(1)}, f32[16,128]{1,0:T(8,128)S(1)}, f32[16,32]{1,0:T(8,128)S(1)}, f32[16,16]{1,0:T(8,128)S(1)}) custom-call(f32[16,40,256]{2,1,0:T(8,128)S(1)} %all_to_all.47.refs_0_), custom_call_target="tpu_custom_call" | custom-call | tf_op jit(solution)/shard_map/pallas_call | solution.py:315
  107.4 13.0 %all_to_all.48.ag.ag1 = f32[16,16,256]{2,1,0:T(8,128)S(1)} all-to-all(f32[16,16,256]{2,1,0:T(8,128)S(1)} %get-tuple-element.33), channel_id=1, replica_groups=mesh['sta'=16,'cel'=16] {'cel'}, dimensions={0} | all-to-all | bytes 524288 | tf_op jit(solution)/shard_map/all_to_all | solution.py:330
  120.4 0.0 copy-done.8
  120.4 0.0 copy-start.5
  120.4 10.2 %shard_map.115 = f32[16,32,128]{2,1,0:T(8,128)S(1)} custom-call(f32[16,16,256]{2,1,0:T(8,128)S(1)} %all_to_all.48.ag.ag1, bf16[64,4096]{1,0:T(8,128)(2,1)S(1)} %get-tuple-element.34.left_rows, f32[1,2048]{1,0:T(1,128)S(1)} %bitcast.5, bf16[1024,4096]{1,0:T(8,128)(2,1)S(1)} %get-tuple-element.29.refs_0_, bf16[1024,4096]{1,0:T(8,128)(2,1)S(1)} %get-tuple-element.30.refs_1_, ...), custom_call_target="tpu_custom_call" | custom-call | tf_op jit(solution)/shard_map/pallas_call | solution.py:315
  130.6 15.3 %all_to_all.49.refs_0_ = f32[16,32,128]{2,1,0:T(8,128)S(1)} all-to-all(f32[16,32,128]{2,1,0:T(8,128)S(1)} %shard_map.115), channel_id=1, replica_groups=mesh['sta'=16,'cel'=16] {'sta'}, dimensions={0} | all-to-all | bytes 524288 | tf_op jit(solution)/shard_map/all_to_all | solution.py:330
  145.9 2.5 %shard_map.116 = (f32[16,16,128]{2,1,0:T(8,128)S(1)}, f32[16,48]{1,0:T(8,128)S(1)}, f32[16,16]{1,0:T(8,128)S(1)}) custom-call(f32[16,32,128]{2,1,0:T(8,128)S(1)} %all_to_all.49.refs_0_, f32[48,128]{1,0:T(8,128)S(1)} %get-tuple-element.35.refs_1_), custom_call_target="tpu_custom_call" | custom-call | tf_op jit(solution)/shard_map/pallas_call | solution.py:315
  148.3 11.0 %all_to_all.50.ag2.refs_6_ = f32[16,16,128]{2,1,0:T(8,128)S(1)} all-to-all(f32[16,16,128]{2,1,0:T(8,128)S(1)} %get-tuple-element.36), channel_id=1, replica_groups=mesh['sta'=16,'cel'=16] {'sta'}, dimensions={0} | all-to-all | bytes 262144 | tf_op jit(solution)/shard_map/all_to_all | solution.py:330
  159.4 0.0 copy-done.5
  159.4 0.0 copy-start.1
  159.4 0.0 copy-start.3
  159.4 6.5 %shard_map.117 = (f32[16,2048]{1,0:T(8,128)S(1)}, f32[16,24,256]{2,1,0:T(8,128)S(1)}) custom-call(f32[16,16,128]{2,1,0:T(8,128)S(1)} %all_to_all.50.ag2.refs_6_, f32[16,16,128]{2,1,0:T(8,128)S(1)} %all_to_all.46.ag.ag0, f32[16,2048]{1,0:T(8,128)S(1)} %copy-done.5, f32[1,2048]{1,0:T(1,128)S(1)} %bitcast.6, f32[16,32]{1,0:T(8,128)S(1)} %get-tuple-element.37.t1, ...), custom_call_target="tpu_custom_call" | custom-call | tf_op jit(solution)/shard_map/pallas_call | solution.py:315
  165.9 14.9 %all_to_all.51.refs_0_ = f32[16,24,256]{2,1,0:T(8,128)S(1)} all-to-all(f32[16,24,256]{2,1,0:T(8,128)S(1)} %get-tuple-element.38), channel_id=1, replica_groups=mesh['sta'=16,'cel'=16] {'cel'}, dimensions={0} | all-to-all | bytes 786432 | tf_op jit(solution)/shard_map/all_to_all | solution.py:330
  180.8 2.6 %shard_map.118 = (f32[16,16,256]{2,1,0:T(8,128)S(1)}, f32[16,48]{1,0:T(8,128)S(1)}, f32[16,16]{1,0:T(8,128)S(1)}) custom-call(f32[16,24,256]{2,1,0:T(8,128)S(1)} %all_to_all.51.refs_0_, f32[32,256]{1,0:T(8,128)S(1)} %get-tuple-element.39.refs_1_, f32[16,128]{1,0:T(8,128)S(1)} %get-tuple-element.40.refs_2_), custom_call_target="tpu_custom_call" | custom-call | tf_op jit(solution)/shard_map/pallas_call | solution.py:315
  183.4 13.8 %all_to_all.52.ag3.refs_2_ = f32[16,16,256]{2,1,0:T(8,128)S(1)} all-to-all(f32[16,16,256]{2,1,0:T(8,128)S(1)} %get-tuple-element.41), channel_id=1, replica_groups=mesh['sta'=16,'cel'=16] {'cel'}, dimensions={0} | all-to-all | bytes 524288 | tf_op jit(solution)/shard_map/all_to_all | solution.py:330
  197.2 0.0 copy-done.1
  197.2 0.0 copy-done.3
  197.2 1.1 shard_map.119
  198.3 13.4 %all_to_all.53.refs_0_ = f32[16,16,128]{2,1,0:T(8,128)S(1)} all-to-all(f32[16,16,128]{2,1,0:T(8,128)S(1)} %get-tuple-element.43), channel_id=1, replica_groups=mesh['sta'=16,'cel'=16] {'sta'}, dimensions={0} | all-to-all | bytes 262144 | tf_op jit(solution)/shard_map/all_to_all | solution.py:330
  211.7 4.2 %shard_map.120 = (f32[2,16,2048]{2,1,0:T(8,128)}, f32[16,4096]{1,0:T(8,128)}, f32[2,16,16]{2,1,0:T(8,128)}, f32[2,16,16]{2,1,0:T(8,128)}) custom-call(f32[16,16,128]{2,1,0:T(8,128)S(1)} %all_to_all.53.refs_0_, f32[48,128]{1,0:T(8,128)S(1)} %get-tuple-element.35.refs_1_, f32[16,16,256]{2,1,0:T(8,128)S(1)} %all_to_all.52.ag3.refs_2_, ...), custom_call_target="tpu_custom_call" | custom-call | tf_op jit(solution)/shard_map/pallas_call | solution.py:315
  (1 shorter events, 0.0 us)
Async XLA Ops:
  0.6 1.0 copy-start
  1.6 0.9 copy-start.2
  2.5 0.7 copy-start.6
  3.2 0.8 copy-start.9
  4.0 0.7 copy-start.10
  4.7 0.7 copy-start.11
  5.4 0.7 copy-start.12
  70.8 0.9 copy-start.4
  71.7 0.7 copy-start.7
  72.4 48.0 %copy-start.8 = (f32[2048]{0:T(1024)S(1)}, f32[2048]{0:T(1024)}, u32[]{:S(2)}) copy-start(f32[2048]{0:T(1024)} %param.12) | copy-start | bytes 24580
  120.4 39.0 %copy-start.5 = (f32[16,2048]{1,0:T(8,128)S(1)}, f32[16,2048]{1,0:T(8,128)}, u32[]{:S(2)}) copy-start(f32[16,2048]{1,0:T(8,128)} %refs_7_.1) | copy-start | bytes 393220
  159.4 37.8 %copy-start.1 = (f32[16,4096]{1,0:T(8,128)S(1)}, f32[16,4096]{1,0:T(8,128)}, u32[]{:S(2)}) copy-start(f32[16,4096]{1,0:T(8,128)} %refs_3_.1) | copy-start | bytes 786436
  159.4 37.8 %copy-start.3 = (f32[16,4096]{1,0:T(8,128)S(1)}, f32[16,4096]{1,0:T(8,128)}, u32[]{:S(2)}) copy-start(f32[16,4096]{1,0:T(8,128)} %refs_4_.1) | copy-start | bytes 786436

commit v2 on v1

--- a/solution.py
+++ b/solution.py
@@ -111,63 +111,86 @@
 
 
 PARTS = 2
-
-
-def first_pass(sp, sh, cp, cd, rho, lb, ln, *refs):
-    matrix, (out, rows, st, ce, cxb, cyb, czb) = refs[: 2 * PARTS], refs[2 * PARTS :]
-    n_s, n_c = st.shape[1], ce.shape[1]
-    st[0:2, :] = sp[...].astype(F32)
-    st[2:3, :] = sh[...].astype(F32) + 0.5
-    ce[...] = jnp.zeros_like(ce)
-    ce[0:2, :] = cp[...].astype(F32)
-    ce[2:3, :] = cd[...].astype(F32)
-    rows[...] = stack_of(ln[...], lb[...])
+LARGE = 62
+
+
+def pieces(x):
+    first = x.astype(BF16).astype(F32)
+    second = (x - first).astype(BF16).astype(F32)
+    return [first, second, x - first - second]
+
+
+def fetch(*refs):
+    count = len(refs) // 2
+    sems = refs[-1]
+    moves = [pltpu.make_async_copy(refs[k], refs[count + k], sems.at[k]) for k in range(count)]
+    for move in moves:
+        move.start()
+    for move in moves:
+        move.wait()
+
+
+def first_pass(sp_v, sh_v, cp_v, cd_v, rho_v, lb_v, ln_v, *refs):
+    matrix, refs = refs[: 2 * PARTS], refs[2 * PARTS :]
+    out, rows, sz_v, czb, a_ref, b_ref, square = refs
+    n_s, n_c = sp_v.shape[1], cp_v.shape[1]
+
+    sx, sy = sp_v[0:1, :].astype(F32), sp_v[1:2, :].astype(F32)
+    sz = sh_v[...].astype(F32) + 0.5
+    sz_v[...] = jnp.broadcast_to(sz, sz_v.shape)
+    one, zero = jnp.ones_like(sx), jnp.zeros_like(sx)
+    b_rows = pieces(sx * sx + sy * sy + sz * sz) + [one, one, one, -2.0 * sx, -2.0 * sy, 2.0 * sz] + [zero] * 7
+    b_ref[...] = jnp.concatenate(b_rows, axis=0).astype(BF16)
+
+    rows[...] = stack_of(ln_v[...], lb_v[...])
     gram = products(rows[...], rows[...])
     stats = lanes([gram[16:, 16:], gram[:16, 16:], gram[:16, :16]], 128)
 
-    def both(ref, r0):
-        return jnp.concatenate([ref[r0 : r0 + 8, :]] * 2, axis=1)
+    def prepare(c0):
+        for half in range(2):
+            here = pl.ds(pl.multiple_of(c0 + 128 * half, 128), 128)
+            put = slice(128 * half, 128 * half + 128)
+            cx, cy = cp_v[0:1, here].astype(F32), cp_v[1:2, here].astype(F32)
+            cz = cd_v[0:1, here].astype(F32)
+            unit, none = jnp.ones_like(cx), jnp.zeros_like(cx)
+            a_rows = [unit, unit, unit] + pieces(cx * cx + cy * cy + cz * cz) + [cx, cy, cz] + [none] * 7
+            turned = jnp.transpose(jnp.concatenate(a_rows, axis=0))
+            a_ref[put, :] = turned.astype(BF16)
+            czb[put, :] = jnp.broadcast_to(turned[:, 8:9], (128, 128))
 
     def cell_block(part, cb, carry):
         hi_ref, lo_ref = matrix[2 * part], matrix[2 * part + 1]
         g0 = pl.multiple_of(cb * TILE, TILE)
-        c0 = part * (n_c // PARTS) + g0
-        for half in range(2):
-            turned = jnp.transpose(ce[:, pl.ds(pl.multiple_of(c0 + 128 * half, 128), 128)])
-            put = slice(128 * half, 128 * half + 128)
-            cxb[put, :] = jnp.broadcast_to(turned[:, 0:1], (128, 128))
-            cyb[put, :] = jnp.broadcast_to(turned[:, 1:2], (128, 128))
-            czb[put, :] = jnp.broadcast_to(turned[:, 2:3], (128, 128))
+        c0 = pl.multiple_of(part * (n_c // PARTS) + g0, TILE)
 
         def station_block(sb, inner):
-            here = pl.ds(pl.multiple_of(sb * TILE, TILE), TILE)
-            sx = jnp.broadcast_to(st[0:1, here], (8, TILE))
-            sy = jnp.broadcast_to(st[1:2, here], (8, TILE))
-            sz = jnp.broadcast_to(st[2:3, here], (8, TILE))
-            for r0 in range(0, TILE, 8):
-                dx = sx - both(cxb, r0)
-                dy = sy - both(cyb, r0)
-                dz = sz + both(czb, r0)
-                dz2 = dz * dz
-                inv = lax.rsqrt(dx * dx + dy * dy + dz2)
-                inv2 = inv * inv
-                g = (dz2 * inv2 - (1.0 / 3.0)) * (inv2 * inv)
-                g_hi = g.astype(BF16)
-                where = pl.ds(pl.multiple_of(g0 + r0, 8), 8)
-                hi_ref[where, here] = g_hi
-                lo_ref[where, here] = (g - g_hi.astype(F32)).astype(BF16)
+            for half in range(2):
+                here = pl.ds(pl.multiple_of(sb * 2 * TILE + half * TILE, TILE), TILE)
+                height = sz_v[:, here]
+                for r0 in range(0, TILE, 8):
+                    dz = height + jnp.concatenate([czb[r0 : r0 + 8, :]] * 2, axis=1)
+                    inv = lax.rsqrt(square[r0 : r0 + 8, here])
+                    inv2 = inv * inv
+                    g = (dz * dz * inv2 - (1.0 / 3.0)) * (inv2 * inv)
+                    where = pl.ds(pl.multiple_of(g0 + r0, 8), 8)
+                    hi_ref[where, here] = g.astype(BF16)
+                    lo_ref[where, here] = (g - hi_ref[where, here].astype(F32)).astype(BF16)
             return inner
 
-        lax.fori_loop(0, n_s // TILE, station_block, 0)
+        lax.fori_loop(0, n_s // (2 * TILE), station_block, 0)
+        prepare(jnp.minimum(c0 + TILE, n_c - TILE))
         big = bdot(rows[...], hi_ref[pl.ds(g0, TILE), :], NT)
         small = bdot(rows[:32, :], lo_ref[pl.ds(g0, TILE), :], NT)
-        total = (big[:32] + big[32:] + small) * (12.0 * rho[0:1, pl.ds(pl.multiple_of(c0, TILE), TILE)])
+        total = (big[:32] + big[32:] + small) * (12.0 * rho_v[0:1, pl.ds(c0, TILE)])
         for k in range(2):
             piece = 2 * cb + k + part * (n_c // PARTS // 128)
             out[piece, :32, :] = total[:, 128 * k : 128 * k + 128]
             out[piece, 32:, :] = stats
+        square[...] = bdot(a_ref[...], b_ref[...])
         return carry
 
+    prepare(0)
+    square[...] = bdot(a_ref[...], b_ref[...])
     for part in range(PARTS):
         lax.fori_loop(0, n_c // PARTS // TILE, functools.partial(cell_block, part), 0)
 
@@ -310,12 +333,12 @@
     betas[1] = lower
 
 
-def call(kernel, args, outs, scratch=(), limit=4):
+def call(kernel, args, outs, scratch=(), limit=4, where=pltpu.VMEM):
     spec = pl.BlockSpec(memory_space=pltpu.VMEM)
     return pl.pallas_call(
         kernel,
         out_shape=tuple(outs),
-        in_specs=[spec] * len(args),
+        in_specs=[pl.BlockSpec(memory_space=where)] * len(args),
         out_specs=tuple(spec for _ in outs),
         scratch_shapes=list(scratch),
         compiler_params=pltpu.CompilerParams(vmem_limit_bytes=limit * 2**20),
@@ -335,21 +358,29 @@
     n_sta, n_cel = lax.axis_size("sta"), lax.axis_size("cel")
     stations, cells = n_s * n_sta, n_c * n_cel
     cp, sp = n_c // n_sta, n_s // n_cel
-    lb, ln, q = left_before, left_now, right_before
-    rho = cell_density.reshape(1, n_c)
     small = f32(16, 16)
 
+    inputs = (
+        station_plane,
+        station_height.reshape(1, n_s),
+        cell_plane,
+        cell_depth.reshape(1, n_c),
+        cell_density.reshape(1, n_c),
+        left_before,
+        left_now,
+        right_before,
+    )
+    sp_v, sh_v, cp_v, cd_v, rho, lb, ln, q = call(
+        fetch,
+        inputs,
+        [pltpu.VMEM(v.shape, v.dtype) for v in inputs],
+        [pltpu.SemaphoreType.DMA((len(inputs),))],
+        limit=LARGE,
+        where=pltpu.HBM,
+    )
     *matrix, rs0, left_rows = call(
         first_pass,
-        (
-            station_plane,
-            station_height.reshape(1, n_s),
-            cell_plane,
-            cell_depth.reshape(1, n_c),
-            rho,
-            lb,
-            ln,
-        ),
+        (sp_v, sh_v, cp_v, cd_v, rho, lb, ln),
         (
             *[pltpu.VMEM((n_c // PARTS, n_s), BF16)] * (2 * PARTS),
             f32(n_sta, 48, cp),
@@ -357,11 +388,12 @@
         ),
         [
             pltpu.VMEM((8, n_s), F32),
-            pltpu.VMEM((8, n_c), F32),
             pltpu.VMEM((TILE, 128), F32),
-            pltpu.VMEM((TILE, 128), F32),
-            pltpu.VMEM((TILE, 128), F32),
+            pltpu.VMEM((TILE, 16), BF16),
+            pltpu.VMEM((16, n_s), BF16),
+            pltpu.VMEM((TILE, n_s), F32),
         ],
+        limit=10,
     )
     ag0, keep0 = call(first_sum, (exchange(rs0, "sta"),), (f32(n_sta, 16, cp), f32(48, cp)))
     ag0 = exchange(ag0, "sta")

time: 217 us -> 204 us (0.940)
  local copies, waits for them, and re-layouts: 7.09 us -> 0 us
  Pallas kernels: 71.8 us -> 66.5 us
    unnamed x26 -> x0, local copies, waits for them, and re-layouts: 7.09 us -> none
    pallas_call x10 -> x11, Pallas kernels: 71.8 us -> 66.5 us  [call(): pl.pallas_call(kernel, out_shape=tuple(outs), in_specs=[pl.BlockSpec(memo...]
where the time goes in v2:
time: 204 us; the launch traced here: 203 us
  blocking collectives  136 us (67%)
  Pallas kernels  66.5 us (33%)
    all_to_all x9, blocking collectives, exchange(): return lax.all_to_all(value, axis, split_axis=0, concat_axis=0, tiled=True)  136 us
    pallas_call x11, Pallas kernels, call(): pl.pallas_call(kernel, out_shape=tuple(outs), in_specs=[pl.BlockSpec(memo...  66.5 us

profile of v2, /device:TPU:1, one launch (start us, length us, event | category | flops | bytes accessed | tf_op | source)
XLA Modules:
  0.0 203.5 jit_solution(8021920070997075079)
XLA Ops:
  0.6 1.2 shard_map.111
  1.9 28.7 %shard_map.112 = (bf16[1024,4096]{1,0:T(8,128)(2,1)S(1)}, bf16[1024,4096]{1,0:T(8,128)(2,1)S(1)}, bf16[1024,4096]{1,0:T(8,128)(2,1)S(1)}, bf16[1024,4096]{1,0:T(...) custom-call(s32[2,4096]{1,0:T(2,128)S(1)} %get-tuple-element.35.sp_v, ...), custom_call_target="tpu_custom_call" | custom-call | tf_op jit(solution)/shard_map/pallas_call | solution.py:338
  30.6 18.0 %all_to_all.45.rs = f32[16,48,128]{2,1,0:T(8,128)S(1)} all-to-all(f32[16,48,128]{2,1,0:T(8,128)S(1)} %get-tuple-element.42), channel_id=1, replica_groups=mesh['sta'=16,'cel'=16] {'sta'}, dimensions={0} | all-to-all | bytes 786432 | tf_op jit(solution)/shard_map/all_to_all | solution.py:353
  48.6 11.4 %all_to_all.46.ag.ag0 = f32[16,16,128]{2,1,0:T(8,128)S(1)} all-to-all(f32[16,16,128]{2,1,0:T(8,128)S(1)} %get-tuple-element.43), channel_id=1, replica_groups=mesh['sta'=16,'cel'=16] {'sta'}, dimensions={0} | all-to-all | bytes 262144 | tf_op jit(solution)/shard_map/all_to_all | solution.py:353
  59.9 7.2 %shard_map.114 = f32[16,40,256]{2,1,0:T(8,128)S(1)} custom-call(f32[16,16,128]{2,1,0:T(8,128)S(1)} %all_to_all.46.ag.ag0, f32[16,2048]{1,0:T(8,128)S(1)} %get-tuple-element.44.q.refs_7_, f32[1,2048]{1,0:T(1,128)S(1)} %get-tuple-element.39.rho_v.rho, bf16[1024,4096]{1,0:T(8,128)(2,1)S(1)} %get-tuple-element.45.refs_0_, ...), custom_call_target="tpu_custom_call" | custom-call | tf_op jit(solution)/shard_map/pallas_call | solution.py:338
  67.1 25.5 %all_to_all.47.refs_0_ = f32[16,40,256]{2,1,0:T(8,128)S(1)} all-to-all(f32[16,40,256]{2,1,0:T(8,128)S(1)} %shard_map.114), channel_id=1, replica_groups=mesh['sta'=16,'cel'=16] {'cel'}, dimensions={0} | all-to-all | bytes 1310720 | tf_op jit(solution)/shard_map/all_to_all | solution.py:353
  92.7 2.3 %shard_map.115 = (f32[16,16,256]{2,1,0:T(8,128)S(1)}, f32[32,256]{1,0:T(8,128)S(1)}, f32[16,128]{1,0:T(8,128)S(1)}, f32[16,32]{1,0:T(8,128)S(1)}, f32[16,16]{1,0:T(8,128)S(1)}) custom-call(f32[16,40,256]{2,1,0:T(8,128)S(1)} %all_to_all.47.refs_0_), custom_call_target="tpu_custom_call" | custom-call | tf_op jit(solution)/shard_map/pallas_call | solution.py:338
  94.9 13.0 %all_to_all.48.ag.ag1 = f32[16,16,256]{2,1,0:T(8,128)S(1)} all-to-all(f32[16,16,256]{2,1,0:T(8,128)S(1)} %get-tuple-element.49), channel_id=1, replica_groups=mesh['sta'=16,'cel'=16] {'cel'}, dimensions={0} | all-to-all | bytes 524288 | tf_op jit(solution)/shard_map/all_to_all | solution.py:353
  108.0 10.2 %shard_map.116 = f32[16,32,128]{2,1,0:T(8,128)S(1)} custom-call(f32[16,16,256]{2,1,0:T(8,128)S(1)} %all_to_all.48.ag.ag1, bf16[64,4096]{1,0:T(8,128)(2,1)S(1)} %get-tuple-element.50.left_rows, f32[1,2048]{1,0:T(1,128)S(1)} %get-tuple-element.39.rho_v.rho, bf16[1024,4096]{1,0:T(8,128)(2,1)S(1)} %get-tuple-element.45.refs_0_, ...), custom_call_target="tpu_custom_call" | custom-call | tf_op jit(solution)/shard_map/pallas_call | solution.py:338
  118.1 15.3 %all_to_all.49.refs_0_ = f32[16,32,128]{2,1,0:T(8,128)S(1)} all-to-all(f32[16,32,128]{2,1,0:T(8,128)S(1)} %shard_map.116), channel_id=1, replica_groups=mesh['sta'=16,'cel'=16] {'sta'}, dimensions={0} | all-to-all | bytes 524288 | tf_op jit(solution)/shard_map/all_to_all | solution.py:353
  133.4 2.5 %shard_map.117 = (f32[16,16,128]{2,1,0:T(8,128)S(1)}, f32[16,48]{1,0:T(8,128)S(1)}, f32[16,16]{1,0:T(8,128)S(1)}) custom-call(f32[16,32,128]{2,1,0:T(8,128)S(1)} %all_to_all.49.refs_0_, f32[48,128]{1,0:T(8,128)S(1)} %get-tuple-element.51.refs_1_), custom_call_target="tpu_custom_call" | custom-call | tf_op jit(solution)/shard_map/pallas_call | solution.py:338
  135.9 11.0 %all_to_all.50.ag2.refs_6_ = f32[16,16,128]{2,1,0:T(8,128)S(1)} all-to-all(f32[16,16,128]{2,1,0:T(8,128)S(1)} %get-tuple-element.52), channel_id=1, replica_groups=mesh['sta'=16,'cel'=16] {'sta'}, dimensions={0} | all-to-all | bytes 262144 | tf_op jit(solution)/shard_map/all_to_all | solution.py:353
  146.9 6.5 %shard_map.118 = (f32[16,2048]{1,0:T(8,128)S(1)}, f32[16,24,256]{2,1,0:T(8,128)S(1)}) custom-call(f32[16,16,128]{2,1,0:T(8,128)S(1)} %all_to_all.50.ag2.refs_6_, f32[16,16,128]{2,1,0:T(8,128)S(1)} %all_to_all.46.ag.ag0, f32[16,2048]{1,0:T(8,128)S(1)} %get-tuple-element.44.q.refs_7_, f32[1,2048]{1,0:T(1,128)S(1)} %get-tuple-element.39.rho_v.rho, ...), custom_call_target="tpu_custom_call" | custom-call | tf_op jit(solution)/shard_map/pallas_call | solution.py:338
  153.4 14.9 %all_to_all.51.refs_0_ = f32[16,24,256]{2,1,0:T(8,128)S(1)} all-to-all(f32[16,24,256]{2,1,0:T(8,128)S(1)} %get-tuple-element.54), channel_id=1, replica_groups=mesh['sta'=16,'cel'=16] {'cel'}, dimensions={0} | all-to-all | bytes 786432 | tf_op jit(solution)/shard_map/all_to_all | solution.py:353
  168.3 2.6 %shard_map.119 = (f32[16,16,256]{2,1,0:T(8,128)S(1)}, f32[16,48]{1,0:T(8,128)S(1)}, f32[16,16]{1,0:T(8,128)S(1)}) custom-call(f32[16,24,256]{2,1,0:T(8,128)S(1)} %all_to_all.51.refs_0_, f32[32,256]{1,0:T(8,128)S(1)} %get-tuple-element.55.refs_1_, f32[16,128]{1,0:T(8,128)S(1)} %get-tuple-element.56.refs_2_), custom_call_target="tpu_custom_call" | custom-call | tf_op jit(solution)/shard_map/pallas_call | solution.py:338
  170.9 13.8 %all_to_all.52.ag3.refs_2_ = f32[16,16,256]{2,1,0:T(8,128)S(1)} all-to-all(f32[16,16,256]{2,1,0:T(8,128)S(1)} %get-tuple-element.57), channel_id=1, replica_groups=mesh['sta'=16,'cel'=16] {'cel'}, dimensions={0} | all-to-all | bytes 524288 | tf_op jit(solution)/shard_map/all_to_all | solution.py:353
  184.7 1.1 shard_map.120
  185.8 13.4 %all_to_all.53.refs_0_ = f32[16,16,128]{2,1,0:T(8,128)S(1)} all-to-all(f32[16,16,128]{2,1,0:T(8,128)S(1)} %get-tuple-element.59), channel_id=1, replica_groups=mesh['sta'=16,'cel'=16] {'sta'}, dimensions={0} | all-to-all | bytes 262144 | tf_op jit(solution)/shard_map/all_to_all | solution.py:353
  199.2 4.3 %shard_map.121 = (f32[2,16,2048]{2,1,0:T(8,128)}, f32[16,4096]{1,0:T(8,128)}, f32[2,16,16]{2,1,0:T(8,128)}, f32[2,16,16]{2,1,0:T(8,128)}) custom-call(f32[16,16,128]{2,1,0:T(8,128)S(1)} %all_to_all.53.refs_0_, f32[48,128]{1,0:T(8,128)S(1)} %get-tuple-element.51.refs_1_, f32[16,16,256]{2,1,0:T(8,128)S(1)} %all_to_all.52.ag3.refs_2_, ...), custom_call_target="tpu_custom_call" | custom-call | tf_op jit(solution)/shard_map/pallas_call | solution.py:338
  (1 shorter events, 0.0 us)

commit v3 on v2

--- a/solution.py
+++ b/solution.py
@@ -40,11 +40,15 @@
 
 
 def wide(stats):
-    return jnp.concatenate([stats[:8], stats[8:]], axis=1)
-
-
-def tall(stats):
-    return jnp.concatenate([stats[:, :128], stats[:, 128:]], axis=0)
+    return lanes([stats[:8], stats[8:]], 128)
+
+
+def tall(tile):
+    return jnp.concatenate([tile[:, :48], tile[:, 48:96]], axis=0)
+
+
+def unfolded(message, count):
+    return jnp.concatenate([message[:, 256 * k : 256 * k + 256] for k in range(count // 8)], axis=0)
 
 
 def factor(gram):
@@ -132,7 +136,7 @@
 
 def first_pass(sp_v, sh_v, cp_v, cd_v, rho_v, lb_v, ln_v, *refs):
     matrix, refs = refs[: 2 * PARTS], refs[2 * PARTS :]
-    out, rows, sz_v, czb, a_ref, b_ref, square = refs
+    out, rows, stats_out, sz_v, czb, a_ref, b_ref, square = refs
     n_s, n_c = sp_v.shape[1], cp_v.shape[1]
 
     sx, sy = sp_v[0:1, :].astype(F32), sp_v[1:2, :].astype(F32)
@@ -144,7 +148,7 @@
 
     rows[...] = stack_of(ln_v[...], lb_v[...])
     gram = products(rows[...], rows[...])
-    stats = lanes([gram[16:, 16:], gram[:16, 16:], gram[:16, :16]], 128)
+    stats_out[...] = lanes([gram[16:, 16:], gram[:16, 16:], gram[:16, :16]], 128)
 
     def prepare(c0):
         for half in range(2):
@@ -184,8 +188,7 @@
         total = (big[:32] + big[32:] + small) * (12.0 * rho_v[0:1, pl.ds(c0, TILE)])
         for k in range(2):
             piece = 2 * cb + k + part * (n_c // PARTS // 128)
-            out[piece, :32, :] = total[:, 128 * k : 128 * k + 128]
-            out[piece, 32:, :] = stats
+            out[piece] = total[:, 128 * k : 128 * k + 128]
         square[...] = bdot(a_ref[...], b_ref[...])
         return carry
 
@@ -202,8 +205,9 @@
 
 
 def forward_product(rows, count, matrix, out, stats):
-    step = 2 * TILE
+    step = 4 * TILE
     size = matrix[0].shape[0]
+    tile = wide(stats)
 
     def station_block(sb, carry):
         s0 = pl.multiple_of(sb * step, step)
@@ -213,9 +217,11 @@
             big = bdot(rows[:, own], matrix[2 * part][:, pl.ds(s0, step)])
             small = bdot(rows[:count, own], matrix[2 * part + 1][:, pl.ds(s0, step)])
             total = total + (big[:count] + big[count:] + small)
-        for k in range(2):
-            out[2 * sb + k, :count, :] = total[:, TILE * k : TILE * k + TILE]
-            out[2 * sb + k, count:, :] = stats
+        for k in range(step // TILE):
+            piece = sb * (step // TILE) + k
+            for r in range(count // 8):
+                out[piece, :, 256 * r : 256 * r + 256] = total[8 * r : 8 * r + 8, TILE * k : TILE * k + TILE]
+            out[piece, :, 32 * count :] = tile
         return carry
 
     lax.fori_loop(0, matrix[0].shape[1] // step, station_block, 0)
@@ -229,51 +235,60 @@
     rows[...] = stack_of(w * scale, base * scale)
     pair = stack_of(w, base)
     gram = products(pair, pair)
-    stats = lanes([gram[16:, 16:], gram[:16, 16:], gram[:16, :16]], 128)
-    forward_product(rows, 32, matrix, out, wide(stats))
+    stats = jnp.concatenate([gram[16:, 16:], gram[:16, 16:], gram[:16, :16]], axis=1)
+    forward_product(rows, 32, matrix, out, stats)
+
+
+def pair_sum(rs, out):
+    half = out.shape[0]
+    for k in range(half):
+        out[k] = rs[k] + rs[half + k]
 
 
 def second_sum(cells, rs, ag, keep, stats_out, t_out, l_out):
     total = added(rs)
-    stats = tall(total[32:]) * (1.0 / cells)
-    stats_out[...] = stats
+    rows = unfolded(total, 32)
+    stats = tall(total[:, 1024:]) * (1.0 / cells)
+    stats_out[...] = lanes([stats], 128)
     lower, t = orthonormal([block_of(stats, 1)], [[block_of(stats, 0)]], block_of(stats, 2))
     l_out[...] = lower
     t_out[...] = t
-    v = fdot(t, total[:32])
-    keep[...] = jnp.concatenate([v, total[16:32]], axis=0)
+    v = fdot(t, rows)
+    keep[...] = jnp.concatenate([v, rows[16:]], axis=0)
     copies(ag, v)
 
 
-def third_pass(ag, left_rows, rho, *refs):
+def third_pass(ag, left_rows, stats0, rho, *refs):
     matrix, (out, rows) = refs[: 2 * PARTS], refs[2 * PARTS :]
     v = gathered(ag)
     rows[...] = stack_of(v)
     gram = products(rows[...], left_rows[...])
-    stats = lanes([gram[:, 16:], gram[:, :16], products(rows[...], rows[...])], 128)
+    stats = lanes([gram[:, 16:], gram[:, :16], products(rows[...], rows[...]), stats0[:, :48]], 128)
 
     size = matrix[0].shape[0]
+    step = 2 * TILE
 
     def cell_block(part, cb, carry):
-        g0 = pl.multiple_of(cb * TILE, TILE)
-        c0 = pl.multiple_of(part * size + g0, TILE)
-        big = bdot(rows[...], matrix[2 * part][pl.ds(g0, TILE), :], NT)
-        small = bdot(rows[:16, :], matrix[2 * part + 1][pl.ds(g0, TILE), :], NT)
-        total = (big[:16] + big[16:] + small) * (12.0 * rho[0:1, pl.ds(c0, TILE)])
-        for k in range(2):
-            piece = 2 * cb + k + part * (size // 128)
+        g0 = pl.multiple_of(cb * step, step)
+        c0 = pl.multiple_of(part * size + g0, step)
+        big = bdot(rows[...], matrix[2 * part][pl.ds(g0, step), :], NT)
+        small = bdot(rows[:16, :], matrix[2 * part + 1][pl.ds(g0, step), :], NT)
+        total = (big[:16] + big[16:] + small) * (12.0 * rho[0:1, pl.ds(c0, step)])
+        for k in range(step // 128):
+            piece = step // 128 * cb + k + part * (size // 128)
             out[piece, :16, :] = total[:, 128 * k : 128 * k + 128]
             out[piece, 16:, :] = stats
         return carry
 
     for part in range(PARTS):
-        lax.fori_loop(0, size // TILE, functools.partial(cell_block, part), 0)
-
-
-def third_sum(stations, rs, keep0, ag, t_out, l_out):
+        lax.fori_loop(0, size // step, functools.partial(cell_block, part), 0)
+
+
+def third_sum(stations, rs, keep0, ag, base_out, t_out, l_out):
     total = added(rs)
     stats = total[16:] * (1.0 / stations)
-    base = keep0[32:48, :] * (1.0 / stations)
+    base = stats[:, 48:96]
+    base_out[...] = lanes([base], 128)
     grams = [[block_of(base, 0)], [block_of(base, 1), block_of(base, 2)]]
     lower, t = orthonormal([block_of(stats, 0), block_of(stats, 1)], grams, block_of(stats, 2))
     l_out[...] = lower
@@ -282,26 +297,30 @@
     copies(ag, w)
 
 
-def fourth_pass(ag2, ag0, q, rho, t1, *refs):
-    matrix, (right_out, out, rows) = refs[: 2 * PARTS], refs[2 * PARTS :]
+def fourth_pass(ag2, ag0, q, rho, t1, stats1, *refs):
+    matrix, (right_out, own_out, out, rows) = refs[: 2 * PARTS], refs[2 * PARTS :]
     base = q[...]
     right = fdot(t1[...], jnp.concatenate([gathered(ag0), base], axis=0))
     right_out[...] = right
     w = gathered(ag2)
     rows[...] = stack_of(w * (12.0 * rho[...]))
-    gram = products(stack_of(right, w), stack_of(base, right, w))
-    stats = lanes([gram[:16, :32], gram[16:, :48]], 128)
-    forward_product(rows, 16, matrix, out, wide(stats))
-
-
-def fourth_sum(cells, rs, keep1, stats1, ag, t_out, l_out):
+    t_w, t_q = t1[:, :16], t1[:, 16:]
+    qq, wq, ww = block_of(stats1, 0), block_of(stats1, 1), block_of(stats1, 2)
+    with_q = fdot(t_w, wq) + fdot(t_q, qq)
+    with_w = fdot(t_w, ww) + fdot(t_q, wq, NT)
+    own_out[...] = lanes([with_q, fdot(with_w, t_w, NT) + fdot(with_q, t_q, NT)], 128)
+    stats = products(stack_of(w), stack_of(base, right, w))
+    forward_product(rows, 16, matrix, out, stats)
+
+
+def fourth_sum(cells, rs, keep1, stats1, own1, ag, t_out, l_out):
     total = added(rs)
-    stats = tall(total[16:]) * (1.0 / cells)
-    grams = [[block_of(stats1[...], 0)], [block_of(stats, 0), block_of(stats, 1)]]
-    lower, t = orthonormal([block_of(stats, 2), block_of(stats, 3)], grams, block_of(stats, 4))
+    stats = tall(total[:, 512:]) * (1.0 / cells)
+    grams = [[block_of(stats1, 0)], [block_of(own1, 0), block_of(own1, 1)]]
+    lower, t = orthonormal([block_of(stats, 0), block_of(stats, 1)], grams, block_of(stats, 2))
     l_out[...] = lower
     t_out[...] = t
-    v = fdot(t, jnp.concatenate([total[:16], keep1[16:, :], keep1[:16, :]], axis=0))
+    v = fdot(t, jnp.concatenate([unfolded(total, 16), keep1[16:, :], keep1[:16, :]], axis=0))
     copies(ag, v)
 
 
@@ -314,9 +333,8 @@
     copies(out, lanes([gram[:16, :48], gram[16:, :64]], 128))
 
 
-def finish(stations, rs, keep0, ag3, lb, ln, left1, ag2, q, right1, t3, l1, l2, l3, rights, left_out, alphas, betas):
+def finish(stations, rs, base, ag3, lb, ln, left1, ag2, q, right1, t3, l1, l2, l3, rights, left_out, alphas, betas):
     stats = added(rs) * (1.0 / stations)
-    base = keep0[32:48, :] * (1.0 / stations)
     grams = [
         [block_of(base, 0)],
         [block_of(base, 1), block_of(base, 2)],
@@ -349,8 +367,8 @@
     return jax.ShapeDtypeStruct(shape, F32)
 
 
-def exchange(value, axis):
-    return lax.all_to_all(value, axis, split_axis=0, concat_axis=0, tiled=True)
+def exchange(value, axis, groups=None):
+    return lax.all_to_all(value, axis, split_axis=0, concat_axis=0, tiled=True, axis_index_groups=groups)
 
 
 def body(station_plane, station_height, cell_plane, cell_depth, cell_density, left_before, left_now, right_before):
@@ -378,13 +396,14 @@
         limit=LARGE,
         where=pltpu.HBM,
     )
-    *matrix, rs0, left_rows = call(
+    *matrix, rs0, left_rows, stats0 = call(
         first_pass,
         (sp_v, sh_v, cp_v, cd_v, rho, lb, ln),
         (
             *[pltpu.VMEM((n_c // PARTS, n_s), BF16)] * (2 * PARTS),
-            f32(n_sta, 48, cp),
+            f32(n_sta, 32, cp),
             pltpu.VMEM((64, n_s), BF16),
+            f32(16, 128),
         ),
         [
             pltpu.VMEM((8, n_s), F32),
@@ -395,38 +414,42 @@
         ],
         limit=10,
     )
-    ag0, keep0 = call(first_sum, (exchange(rs0, "sta"),), (f32(n_sta, 16, cp), f32(48, cp)))
+    ag0, keep0 = call(first_sum, (exchange(rs0, "sta"),), (f32(n_sta, 16, cp), f32(32, cp)))
     ag0 = exchange(ag0, "sta")
-    (rs1,) = call(second_pass, (ag0, q, rho, *matrix), (f32(n_cel, 40, sp),), [pltpu.VMEM((64, n_c), BF16)])
+    (rs1,) = call(second_pass, (ag0, q, rho, *matrix), (f32(n_cel, 8, 1152),), [pltpu.VMEM((64, n_c), BF16)])
+    half = n_cel // 2
+    across = [[k, half + k] for k in range(half)]
+    along = [[half * side + k for k in range(half)] for side in range(2)]
+    (rs1,) = call(pair_sum, (exchange(rs1, "cel", across),), (f32(half, 8, 1152),))
     ag1, keep1, stats1, t1, l1 = call(
         lambda *refs: second_sum(cells, *refs),
-        (exchange(rs1, "cel"),),
+        (exchange(rs1, "cel", along),),
         (f32(n_cel, 16, sp), f32(32, sp), f32(16, 128), f32(16, 32), small),
     )
     ag1 = exchange(ag1, "cel")
-    (rs2,) = call(third_pass, (ag1, left_rows, rho, *matrix), (f32(n_sta, 32, cp),), [pltpu.VMEM((32, n_s), BF16)])
-    ag2, t2, l2 = call(
+    (rs2,) = call(third_pass, (ag1, left_rows, stats0, rho, *matrix), (f32(n_sta, 32, cp),), [pltpu.VMEM((32, n_s), BF16)])
+    ag2, base2, t2, l2 = call(
         lambda *refs: third_sum(stations, *refs),
         (exchange(rs2, "sta"), keep0),
-        (f32(n_sta, 16, cp), f32(16, 48), small),
+        (f32(n_sta, 16, cp), f32(16, 128), f32(16, 48), small),
     )
     ag2 = exchange(ag2, "sta")
-    right1, rs3 = call(
+    right1, own1, rs3 = call(
         fourth_pass,
-        (ag2, ag0, q, rho, t1, *matrix),
-        (f32(16, n_c), f32(n_cel, 24, sp)),
+        (ag2, ag0, q, rho, t1, stats1, *matrix),
+        (f32(16, n_c), f32(16, 128), f32(n_cel, 8, 640)),
         [pltpu.VMEM((32, n_c), BF16)],
     )
     ag3, t3, l3 = call(
         lambda *refs: fourth_sum(cells, *refs),
-        (exchange(rs3, "cel"), keep1, stats1),
+        (exchange(rs3, "cel"), keep1, stats1, own1),
         (f32(n_cel, 16, sp), f32(16, 48), small),
     )
     ag3 = exchange(ag3, "cel")
     left1, rs4 = call(last_stats, (ag3, ag1, lb, ln, t2), (f32(16, n_s), f32(n_sta, 16, 128)))
     rights, left2, alphas, betas = call(
         lambda *refs: finish(stations, *refs),
-        (exchange(rs4, "sta"), keep0, ag3, lb, ln, left1, ag2, q, right1, t3, l1, l2, l3),
+        (exchange(rs4, "sta"), base2, ag3, lb, ln, left1, ag2, q, right1, t3, l1, l2, l3),
         (f32(2, 16, n_c), f32(16, n_s), f32(2, 16, 16), f32(2, 16, 16)),
     )
     return rights, left2, alphas, betas

time: 204 us -> 202 us (level)
    pallas_call x11 -> x12, Pallas kernels: 66.5 us -> 65.6 us  [call(): pl.pallas_call(kernel, out_shape=tuple(outs), in_specs=[pl.BlockSpec(memo...]
    all_to_all x9 -> x10, blocking collectives: 136 us -> 135 us  [exchange(): lax.all_to_all(value, axis, split_axis=0, concat_axis=0, tiled=True, axis...]
where the time goes in v3:
time: 202 us
  blocking collectives  135 us (67%)
  Pallas kernels  65.6 us (32%)
    all_to_all x10, blocking collectives, exchange(): lax.all_to_all(value, axis, split_axis=0, concat_axis=0, tiled=True, axis...  135 us
    pallas_call x12, Pallas kernels, call(): pl.pallas_call(kernel, out_shape=tuple(outs), in_specs=[pl.BlockSpec(memo...  65.6 us

profile of v3, /device:TPU:1, one launch (start us, length us, event | category | flops | bytes accessed | tf_op | source)
XLA Modules:
  0.0 201.7 jit_solution(13484675318092338218)
XLA Ops:
  0.6 1.2 shard_map.111
  1.9 28.7 %shard_map.112 = (bf16[1024,4096]{1,0:T(8,128)(2,1)S(1)}, bf16[1024,4096]{1,0:T(8,128)(2,1)S(1)}, bf16[1024,4096]{1,0:T(8,128)(2,1)S(1)}, bf16[1024,4096]{1,0:T(...) custom-call(s32[2,4096]{1,0:T(2,128)S(1)} %get-tuple-element.38.sp_v, ...), custom_call_target="tpu_custom_call" | custom-call | tf_op jit(solution)/shard_map/pallas_call | solution.py:356
  30.6 16.9 %all_to_all.50.rs = f32[16,32,128]{2,1,0:T(8,128)S(1)} all-to-all(f32[16,32,128]{2,1,0:T(8,128)S(1)} %get-tuple-element.45), channel_id=1, replica_groups=mesh['sta'=16,'cel'=16] {'sta'}, dimensions={0} | all-to-all | bytes 524288 | tf_op jit(solution)/shard_map/all_to_all | solution.py:371
  47.5 11.0 %all_to_all.51.ag.ag0 = f32[16,16,128]{2,1,0:T(8,128)S(1)} all-to-all(f32[16,16,128]{2,1,0:T(8,128)S(1)} %get-tuple-element.46), channel_id=1, replica_groups=mesh['sta'=16,'cel'=16] {'sta'}, dimensions={0} | all-to-all | bytes 262144 | tf_op jit(solution)/shard_map/all_to_all | solution.py:371
  58.5 6.7 %shard_map.114 = f32[16,8,1152]{2,1,0:T(8,128)S(1)} custom-call(f32[16,16,128]{2,1,0:T(8,128)S(1)} %all_to_all.51.ag.ag0, f32[16,2048]{1,0:T(8,128)S(1)} %get-tuple-element.47.q.refs_7_, f32[1,2048]{1,0:T(1,128)S(1)} %get-tuple-element.42.rho_v.rho, bf16[1024,4096]{1,0:T(8,128)(2,1)S(1)} %get-tuple-element.48.refs_0_, ...), custom_call_target="tpu_custom_call" | custom-call | tf_op jit(solution)/shard_map/pallas_call | solution.py:356
  65.3 10.5 %all_to_all.52.rs = f32[16,8,1152]{2,1,0:T(8,128)S(1)} all-to-all(f32[16,8,1152]{2,1,0:T(8,128)S(1)} %shard_map.114), channel_id=1, replica_groups={{0,8},{1,9},{2,10},{3,11},{4,12},{5,13},{6,14},{7,15},{16,24},{17,25},{..., dimensions={0} | all-to-all | bytes 1179648 | tf_op jit(solution)/shard_map/all_to_all | solution.py:371
  75.8 18.3 %all_to_all.53.refs_0_ = f32[8,8,1152]{2,1,0:T(8,128)S(1)} all-to-all(f32[8,8,1152]{2,1,0:T(8,128)S(1)} %shard_map.115), channel_id=1, replica_groups={{0,1,2,3,4,5,6,7},{8,9,10,11,12,13,14,15},{16,17,18,19,20,21,22,23},{24..., dimensions={0} | all-to-all | bytes 589824 | tf_op jit(solution)/shard_map/all_to_all | solution.py:371
  94.1 2.3 %shard_map.116 = (f32[16,16,256]{2,1,0:T(8,128)S(1)}, f32[32,256]{1,0:T(8,128)S(1)}, f32[16,128]{1,0:T(8,128)S(1)}, f32[16,32]{1,0:T(8,128)S(1)}, f32[16,16]{1,0:T(8,128)S(1)}) custom-call(f32[8,8,1152]{2,1,0:T(8,128)S(1)} %all_to_all.53.refs_0_), custom_call_target="tpu_custom_call" | custom-call | tf_op jit(solution)/shard_map/pallas_call | solution.py:356
  96.5 11.2 %all_to_all.54.ag.ag1 = f32[16,16,256]{2,1,0:T(8,128)S(1)} all-to-all(f32[16,16,256]{2,1,0:T(8,128)S(1)} %get-tuple-element.52), channel_id=1, replica_groups=mesh['sta'=16,'cel'=16] {'cel'}, dimensions={0} | all-to-all | bytes 524288 | tf_op jit(solution)/shard_map/all_to_all | solution.py:371
  107.6 10.1 %shard_map.117 = f32[16,32,128]{2,1,0:T(8,128)S(1)} custom-call(f32[16,16,256]{2,1,0:T(8,128)S(1)} %all_to_all.54.ag.ag1, bf16[64,4096]{1,0:T(8,128)(2,1)S(1)} %get-tuple-element.53.left_rows, f32[16,128]{1,0:T(8,128)S(1)} %get-tuple-element.54.stats0, f32[1,2048]{1,0:T(1,128)S(1)} %get-tuple-element.42.rho_v.rho, ...), custom_call_target="tpu_custom_call" | custom-call | tf_op jit(solution)/shard_map/pallas_call | solution.py:356
  117.8 15.3 %all_to_all.55.refs_0_ = f32[16,32,128]{2,1,0:T(8,128)S(1)} all-to-all(f32[16,32,128]{2,1,0:T(8,128)S(1)} %shard_map.117), channel_id=1, replica_groups=mesh['sta'=16,'cel'=16] {'sta'}, dimensions={0} | all-to-all | bytes 524288 | tf_op jit(solution)/shard_map/all_to_all | solution.py:371
  133.0 2.5 %shard_map.118 = (f32[16,16,128]{2,1,0:T(8,128)S(1)}, f32[16,128]{1,0:T(8,128)S(1)}, f32[16,48]{1,0:T(8,128)S(1)}, f32[16,16]{1,0:T(8,128)S(1)}) custom-call(f32[16,32,128]{2,1,0:T(8,128)S(1)} %all_to_all.55.refs_0_, f32[32,128]{1,0:T(8,128)S(1)} %get-tuple-element.55.refs_1_), custom_call_target="tpu_custom_call" | custom-call | tf_op jit(solution)/shard_map/pallas_call | solution.py:356
  135.5 11.0 %all_to_all.56.ag2.refs_6_ = f32[16,16,128]{2,1,0:T(8,128)S(1)} all-to-all(f32[16,16,128]{2,1,0:T(8,128)S(1)} %get-tuple-element.56), channel_id=1, replica_groups=mesh['sta'=16,'cel'=16] {'sta'}, dimensions={0} | all-to-all | bytes 262144 | tf_op jit(solution)/shard_map/all_to_all | solution.py:371
  146.6 6.1 %shard_map.119 = (f32[16,2048]{1,0:T(8,128)S(1)}, f32[16,128]{1,0:T(8,128)S(1)}, f32[16,8,640]{2,1,0:T(8,128)S(1)}) custom-call(f32[16,16,128]{2,1,0:T(8,128)S(1)} %all_to_all.56.ag2.refs_6_, f32[16,16,128]{2,1,0:T(8,128)S(1)} %all_to_all.51.ag.ag0, f32[16,2048]{1,0:T(8,128)S(1)} %get-tuple-element.47.q.refs_7_, f32[1,2048]{1,0:T(1,128)S(1)} %get-tuple-element.42.rho_v.rho, ...), custom_call_target="tpu_custom_call" | custom-call | tf_op jit(solution)/shard_map/pallas_call | solution.py:356
  152.7 13.7 %all_to_all.57.refs_0_ = f32[16,8,640]{2,1,0:T(8,128)S(1)} all-to-all(f32[16,8,640]{2,1,0:T(8,128)S(1)} %get-tuple-element.59), channel_id=1, replica_groups=mesh['sta'=16,'cel'=16] {'cel'}, dimensions={0} | all-to-all | bytes 655360 | tf_op jit(solution)/shard_map/all_to_all | solution.py:371
  166.3 2.5 %shard_map.120 = (f32[16,16,256]{2,1,0:T(8,128)S(1)}, f32[16,48]{1,0:T(8,128)S(1)}, f32[16,16]{1,0:T(8,128)S(1)}) custom-call(f32[16,8,640]{2,1,0:T(8,128)S(1)} %all_to_all.57.refs_0_, f32[32,256]{1,0:T(8,128)S(1)} %get-tuple-element.60.refs_1_, f32[16,128]{1,0:T(8,128)S(1)} %get-tuple-element.58.stats1.refs_2_, f32[16,128]{1,0:T(8,128)S(1)} %get-tuple-element.61.refs_3_), custom_call_target="tpu_custom_call" | custom-call | tf_op jit(solution)/shard_map/pallas_call | solution.py:356
  168.9 13.5 %all_to_all.58.ag3.refs_2_ = f32[16,16,256]{2,1,0:T(8,128)S(1)} all-to-all(f32[16,16,256]{2,1,0:T(8,128)S(1)} %get-tuple-element.62), channel_id=1, replica_groups=mesh['sta'=16,'cel'=16] {'cel'}, dimensions={0} | all-to-all | bytes 524288 | tf_op jit(solution)/shard_map/all_to_all | solution.py:371
  182.4 1.1 shard_map.121
  183.5 13.9 %all_to_all.59.refs_0_ = f32[16,16,128]{2,1,0:T(8,128)S(1)} all-to-all(f32[16,16,128]{2,1,0:T(8,128)S(1)} %get-tuple-element.64), channel_id=1, replica_groups=mesh['sta'=16,'cel'=16] {'sta'}, dimensions={0} | all-to-all | bytes 262144 | tf_op jit(solution)/shard_map/all_to_all | solution.py:371
  197.5 4.2 %shard_map.122 = (f32[2,16,2048]{2,1,0:T(8,128)}, f32[16,4096]{1,0:T(8,128)}, f32[2,16,16]{2,1,0:T(8,128)}, f32[2,16,16]{2,1,0:T(8,128)}) custom-call(f32[16,16,128]{2,1,0:T(8,128)S(1)} %all_to_all.59.refs_0_, f32[16,128]{1,0:T(8,128)S(1)} %get-tuple-element.65.refs_1_, f32[16,16,256]{2,1,0:T(8,128)S(1)} %all_to_all.58.ag3.refs_2_, ...), custom_call_target="tpu_custom_call" | custom-call | tf_op jit(solution)/shard_map/pallas_call | solution.py:356
  (2 shorter events, 0.1 us)

commit v4 on v3

--- a/solution.py
+++ b/solution.py
@@ -53,23 +53,29 @@
 
 def factor(gram):
     size = gram.shape[0]
-    row = lax.broadcasted_iota(jnp.int32, (size, 1), 0)
-    lane = lax.broadcasted_iota(jnp.int32, (size, size), 1)
-    eye = jnp.where(lax.broadcasted_iota(jnp.int32, (size, size), 0) == lane, 1.0, 0.0)
-    work, inv = gram, eye
-    lower = jnp.zeros_like(gram)
+    row = lax.broadcasted_iota(jnp.int32, (size, 2 * size), 0)
+    lane = lax.broadcasted_iota(jnp.int32, (size, 2 * size), 1)
+    work = jnp.concatenate([gram, jnp.zeros_like(gram)], axis=1)
+    work = work + jnp.where(lane == row + size, 1.0, 0.0)
+    lower = jnp.zeros_like(work)
     for k in range(size):
-        pivot = work[k : k + 1, k : k + 1]
+        column = jnp.broadcast_to(work[:, k : k + 1], work.shape)
+        pivot = column[k : k + 1, :]
         r = lax.rsqrt(pivot)
         r = r * (1.5 - 0.5 * pivot * r * r)
-        col = work[:, k : k + 1] * r
-        lower = jnp.where((lane == k) & (row >= k), col, lower)
-        below = jnp.where(row > k, col, 0.0)
-        work_row = work[k : k + 1, :] * r
-        inv_row = inv[k : k + 1, :] * r
-        work = work - below * work_row
-        inv = jnp.where(row == k, inv_row, inv - below * inv_row)
-    return lower, inv
+        column = column * r
+        lower = jnp.where((lane == k) & (row >= k), column, lower)
+        line = work[k : k + 1, :] * r
+        work = jnp.where(row == k, line, work - jnp.where(row > k, column, 0.0) * line)
+    return lower[:, :size], work[:, size:]
+
+
+def tdot(t, x):
+    t_hi, t_lo = halves(t)
+    x_hi, x_lo = halves(x)
+    size = t.shape[0]
+    big = bdot(jnp.concatenate([t_hi, t_lo], axis=0), x_hi)
+    return big[:size] + (big[size:] + bdot(t_hi, x_lo))
 
 
 def orthonormal(onto, basis, own):
@@ -239,12 +245,6 @@
     forward_product(rows, 32, matrix, out, stats)
 
 
-def pair_sum(rs, out):
-    half = out.shape[0]
-    for k in range(half):
-        out[k] = rs[k] + rs[half + k]
-
-
 def second_sum(cells, rs, ag, keep, stats_out, t_out, l_out):
     total = added(rs)
     rows = unfolded(total, 32)
@@ -300,7 +300,7 @@
 def fourth_pass(ag2, ag0, q, rho, t1, stats1, *refs):
     matrix, (right_out, own_out, out, rows) = refs[: 2 * PARTS], refs[2 * PARTS :]
     base = q[...]
-    right = fdot(t1[...], jnp.concatenate([gathered(ag0), base], axis=0))
+    right = tdot(t1[...], jnp.concatenate([gathered(ag0), base], axis=0))
     right_out[...] = right
     w = gathered(ag2)
     rows[...] = stack_of(w * (12.0 * rho[...]))
@@ -326,7 +326,7 @@
 
 def last_stats(ag3, ag1, lb, ln, t2, left_out, out):
     before, now = lb[...], ln[...]
-    left = fdot(t2[...], jnp.concatenate([gathered(ag1), before, now], axis=0))
+    left = tdot(t2[...], jnp.concatenate([gathered(ag1), before, now], axis=0))
     left_out[...] = left
     v = gathered(ag3)
     gram = products(stack_of(left, v), stack_of(before, now, left, v))
@@ -342,9 +342,9 @@
     ]
     onto = [block_of(stats, 3), block_of(stats, 4), block_of(stats, 5)]
     lower, t = orthonormal(onto, grams, block_of(stats, 6))
-    left_out[...] = fdot(t, jnp.concatenate([gathered(ag3), lb[...], ln[...], left1[...]], axis=0))
+    left_out[...] = tdot(t, jnp.concatenate([gathered(ag3), lb[...], ln[...], left1[...]], axis=0))
     rights[0] = right1[...]
-    rights[1] = fdot(t3[...], jnp.concatenate([gathered(ag2), q[...], right1[...]], axis=0))
+    rights[1] = tdot(t3[...], jnp.concatenate([gathered(ag2), q[...], right1[...]], axis=0))
     alphas[0] = l1[...]
     alphas[1] = l3[...]
     betas[0] = l2[...]
@@ -367,8 +367,8 @@
     return jax.ShapeDtypeStruct(shape, F32)
 
 
-def exchange(value, axis, groups=None):
-    return lax.all_to_all(value, axis, split_axis=0, concat_axis=0, tiled=True, axis_index_groups=groups)
+def exchange(value, axis):
+    return lax.all_to_all(value, axis, split_axis=0, concat_axis=0, tiled=True)
 
 
 def body(station_plane, station_height, cell_plane, cell_depth, cell_density, left_before, left_now, right_before):
@@ -417,13 +417,9 @@
     ag0, keep0 = call(first_sum, (exchange(rs0, "sta"),), (f32(n_sta, 16, cp), f32(32, cp)))
     ag0 = exchange(ag0, "sta")
     (rs1,) = call(second_pass, (ag0, q, rho, *matrix), (f32(n_cel, 8, 1152),), [pltpu.VMEM((64, n_c), BF16)])
-    half = n_cel // 2
-    across = [[k, half + k] for k in range(half)]
-    along = [[half * side + k for k in range(half)] for side in range(2)]
-    (rs1,) = call(pair_sum, (exchange(rs1, "cel", across),), (f32(half, 8, 1152),))
     ag1, keep1, stats1, t1, l1 = call(
         lambda *refs: second_sum(cells, *refs),
-        (exchange(rs1, "cel", along),),
+        (exchange(rs1, "cel"),),
         (f32(n_cel, 16, sp), f32(32, sp), f32(16, 128), f32(16, 32), small),
     )
     ag1 = exchange(ag1, "cel")

time: 202 us -> 199 us (0.985)
  blocking collectives: 135 us -> 132 us
    all_to_all x10 -> x9, blocking collectives: 135 us -> 132 us  [exchange(): return lax.all_to_all(value, axis, split_axis=0, concat_axis=0, tiled=True)]
    pallas_call x12 -> x11, Pallas kernels: 65.6 us -> 65.5 us  [call(): pl.pallas_call(kernel, out_shape=tuple(outs), in_specs=[pl.BlockSpec(memo...]
where the time goes in v4:
time: 199 us; the launch traced here: 198 us
  blocking collectives  132 us (66%)
  Pallas kernels  65.5 us (33%)
    all_to_all x9, blocking collectives, exchange(): return lax.all_to_all(value, axis, split_axis=0, concat_axis=0, tiled=True)  132 us
    pallas_call x11, Pallas kernels, call(): pl.pallas_call(kernel, out_shape=tuple(outs), in_specs=[pl.BlockSpec(memo...  65.5 us

profile of v4, /device:TPU:1, one launch (start us, length us, event | category | flops | bytes accessed | tf_op | source)
XLA Modules:
  0.0 198.4 jit_solution(5171104714432079651)
XLA Ops:
  0.6 1.2 shard_map.111
  1.9 28.7 %shard_map.112 = (bf16[1024,4096]{1,0:T(8,128)(2,1)S(1)}, bf16[1024,4096]{1,0:T(8,128)(2,1)S(1)}, bf16[1024,4096]{1,0:T(8,128)(2,1)S(1)}, bf16[1024,4096]{1,0:T(...) custom-call(s32[2,4096]{1,0:T(2,128)S(1)} %get-tuple-element.38.sp_v, ...), custom_call_target="tpu_custom_call" | custom-call | tf_op jit(solution)/shard_map/pallas_call | solution.py:356
  30.6 16.9 %all_to_all.45.rs = f32[16,32,128]{2,1,0:T(8,128)S(1)} all-to-all(f32[16,32,128]{2,1,0:T(8,128)S(1)} %get-tuple-element.45), channel_id=1, replica_groups=mesh['sta'=16,'cel'=16] {'sta'}, dimensions={0} | all-to-all | bytes 524288 | tf_op jit(solution)/shard_map/all_to_all | solution.py:371
  47.5 11.0 %all_to_all.46.ag.ag0 = f32[16,16,128]{2,1,0:T(8,128)S(1)} all-to-all(f32[16,16,128]{2,1,0:T(8,128)S(1)} %get-tuple-element.46), channel_id=1, replica_groups=mesh['sta'=16,'cel'=16] {'sta'}, dimensions={0} | all-to-all | bytes 262144 | tf_op jit(solution)/shard_map/all_to_all | solution.py:371
  58.5 6.7 %shard_map.114 = f32[16,8,1152]{2,1,0:T(8,128)S(1)} custom-call(f32[16,16,128]{2,1,0:T(8,128)S(1)} %all_to_all.46.ag.ag0, f32[16,2048]{1,0:T(8,128)S(1)} %get-tuple-element.47.q.refs_7_, f32[1,2048]{1,0:T(1,128)S(1)} %get-tuple-element.42.rho_v.rho, bf16[1024,4096]{1,0:T(8,128)(2,1)S(1)} %get-tuple-element.48.refs_0_, ...), custom_call_target="tpu_custom_call" | custom-call | tf_op jit(solution)/shard_map/pallas_call | solution.py:356
  65.3 25.4 %all_to_all.47.refs_0_ = f32[16,8,1152]{2,1,0:T(8,128)S(1)} all-to-all(f32[16,8,1152]{2,1,0:T(8,128)S(1)} %shard_map.114), channel_id=1, replica_groups=mesh['sta'=16,'cel'=16] {'cel'}, dimensions={0} | all-to-all | bytes 1179648 | tf_op jit(solution)/shard_map/all_to_all | solution.py:371
  90.7 2.5 %shard_map.115 = (f32[16,16,256]{2,1,0:T(8,128)S(1)}, f32[32,256]{1,0:T(8,128)S(1)}, f32[16,128]{1,0:T(8,128)S(1)}, f32[16,32]{1,0:T(8,128)S(1)}, f32[16,16]{1,0:T(8,128)S(1)}) custom-call(f32[16,8,1152]{2,1,0:T(8,128)S(1)} %all_to_all.47.refs_0_), custom_call_target="tpu_custom_call" | custom-call | tf_op jit(solution)/shard_map/pallas_call | solution.py:356
  93.2 11.9 %all_to_all.48.ag.ag1 = f32[16,16,256]{2,1,0:T(8,128)S(1)} all-to-all(f32[16,16,256]{2,1,0:T(8,128)S(1)} %get-tuple-element.52), channel_id=1, replica_groups=mesh['sta'=16,'cel'=16] {'cel'}, dimensions={0} | all-to-all | bytes 524288 | tf_op jit(solution)/shard_map/all_to_all | solution.py:371
  105.0 10.1 %shard_map.116 = f32[16,32,128]{2,1,0:T(8,128)S(1)} custom-call(f32[16,16,256]{2,1,0:T(8,128)S(1)} %all_to_all.48.ag.ag1, bf16[64,4096]{1,0:T(8,128)(2,1)S(1)} %get-tuple-element.53.left_rows, f32[16,128]{1,0:T(8,128)S(1)} %get-tuple-element.54.stats0, f32[1,2048]{1,0:T(1,128)S(1)} %get-tuple-element.42.rho_v.rho, ...), custom_call_target="tpu_custom_call" | custom-call | tf_op jit(solution)/shard_map/pallas_call | solution.py:356
  115.2 15.0 %all_to_all.49.refs_0_ = f32[16,32,128]{2,1,0:T(8,128)S(1)} all-to-all(f32[16,32,128]{2,1,0:T(8,128)S(1)} %shard_map.116), channel_id=1, replica_groups=mesh['sta'=16,'cel'=16] {'sta'}, dimensions={0} | all-to-all | bytes 524288 | tf_op jit(solution)/shard_map/all_to_all | solution.py:371
  130.2 2.6 %shard_map.117 = (f32[16,16,128]{2,1,0:T(8,128)S(1)}, f32[16,128]{1,0:T(8,128)S(1)}, f32[16,48]{1,0:T(8,128)S(1)}, f32[16,16]{1,0:T(8,128)S(1)}) custom-call(f32[16,32,128]{2,1,0:T(8,128)S(1)} %all_to_all.49.refs_0_, f32[32,128]{1,0:T(8,128)S(1)} %get-tuple-element.55.refs_1_), custom_call_target="tpu_custom_call" | custom-call | tf_op jit(solution)/shard_map/pallas_call | solution.py:356
  132.9 11.0 %all_to_all.50.ag2.refs_6_ = f32[16,16,128]{2,1,0:T(8,128)S(1)} all-to-all(f32[16,16,128]{2,1,0:T(8,128)S(1)} %get-tuple-element.56), channel_id=1, replica_groups=mesh['sta'=16,'cel'=16] {'sta'}, dimensions={0} | all-to-all | bytes 262144 | tf_op jit(solution)/shard_map/all_to_all | solution.py:371
  143.9 6.0 %shard_map.118 = (f32[16,2048]{1,0:T(8,128)S(1)}, f32[16,128]{1,0:T(8,128)S(1)}, f32[16,8,640]{2,1,0:T(8,128)S(1)}) custom-call(f32[16,16,128]{2,1,0:T(8,128)S(1)} %all_to_all.50.ag2.refs_6_, f32[16,16,128]{2,1,0:T(8,128)S(1)} %all_to_all.46.ag.ag0, f32[16,2048]{1,0:T(8,128)S(1)} %get-tuple-element.47.q.refs_7_, f32[1,2048]{1,0:T(1,128)S(1)} %get-tuple-element.42.rho_v.rho, ...), custom_call_target="tpu_custom_call" | custom-call | tf_op jit(solution)/shard_map/pallas_call | solution.py:356
  149.9 13.8 %all_to_all.51.refs_0_ = f32[16,8,640]{2,1,0:T(8,128)S(1)} all-to-all(f32[16,8,640]{2,1,0:T(8,128)S(1)} %get-tuple-element.59), channel_id=1, replica_groups=mesh['sta'=16,'cel'=16] {'cel'}, dimensions={0} | all-to-all | bytes 655360 | tf_op jit(solution)/shard_map/all_to_all | solution.py:371
  163.7 2.7 %shard_map.119 = (f32[16,16,256]{2,1,0:T(8,128)S(1)}, f32[16,48]{1,0:T(8,128)S(1)}, f32[16,16]{1,0:T(8,128)S(1)}) custom-call(f32[16,8,640]{2,1,0:T(8,128)S(1)} %all_to_all.51.refs_0_, f32[32,256]{1,0:T(8,128)S(1)} %get-tuple-element.60.refs_1_, f32[16,128]{1,0:T(8,128)S(1)} %get-tuple-element.58.stats1.refs_2_, f32[16,128]{1,0:T(8,128)S(1)} %get-tuple-element.61.refs_3_), custom_call_target="tpu_custom_call" | custom-call | tf_op jit(solution)/shard_map/pallas_call | solution.py:356
  166.3 13.5 %all_to_all.52.ag3.refs_2_ = f32[16,16,256]{2,1,0:T(8,128)S(1)} all-to-all(f32[16,16,256]{2,1,0:T(8,128)S(1)} %get-tuple-element.62), channel_id=1, replica_groups=mesh['sta'=16,'cel'=16] {'cel'}, dimensions={0} | all-to-all | bytes 524288 | tf_op jit(solution)/shard_map/all_to_all | solution.py:371
  179.9 0.9 shard_map.120
  180.8 13.5 %all_to_all.53.refs_0_ = f32[16,16,128]{2,1,0:T(8,128)S(1)} all-to-all(f32[16,16,128]{2,1,0:T(8,128)S(1)} %get-tuple-element.64), channel_id=1, replica_groups=mesh['sta'=16,'cel'=16] {'sta'}, dimensions={0} | all-to-all | bytes 262144 | tf_op jit(solution)/shard_map/all_to_all | solution.py:371
  194.3 4.1 %shard_map.121 = (f32[2,16,2048]{2,1,0:T(8,128)}, f32[16,4096]{1,0:T(8,128)}, f32[2,16,16]{2,1,0:T(8,128)}, f32[2,16,16]{2,1,0:T(8,128)}) custom-call(f32[16,16,128]{2,1,0:T(8,128)S(1)} %all_to_all.53.refs_0_, f32[16,128]{1,0:T(8,128)S(1)} %get-tuple-element.65.refs_1_, f32[16,16,256]{2,1,0:T(8,128)S(1)} %all_to_all.52.ag3.refs_2_, ...), custom_call_target="tpu_custom_call" | custom-call | tf_op jit(solution)/shard_map/pallas_call | solution.py:356
  (1 shorter events, 0.0 us)

commit v5 on v4

--- a/solution.py
+++ b/solution.py
@@ -53,21 +53,36 @@
 
 def factor(gram):
     size = gram.shape[0]
-    row = lax.broadcasted_iota(jnp.int32, (size, 2 * size), 0)
-    lane = lax.broadcasted_iota(jnp.int32, (size, 2 * size), 1)
-    work = jnp.concatenate([gram, jnp.zeros_like(gram)], axis=1)
-    work = work + jnp.where(lane == row + size, 1.0, 0.0)
-    lower = jnp.zeros_like(work)
+    shape = (size, 128)
+    row = lax.broadcasted_iota(jnp.int32, shape, 0)
+    lane = lax.broadcasted_iota(jnp.int32, shape, 1)
+    columns = [jnp.broadcast_to(gram[:, k : k + 1], shape) for k in range(size)]
+    inv = jnp.where(lane == row, 1.0, 0.0)
+    lower = jnp.zeros(shape, F32)
     for k in range(size):
-        column = jnp.broadcast_to(work[:, k : k + 1], work.shape)
-        pivot = column[k : k + 1, :]
+        pivot = columns[k][k : k + 1, :]
         r = lax.rsqrt(pivot)
         r = r * (1.5 - 0.5 * pivot * r * r)
-        column = column * r
+        column = columns[k] * r
+        for j in range(k + 1, size):
+            columns[j] = columns[j] - column * column[j : j + 1, :]
         lower = jnp.where((lane == k) & (row >= k), column, lower)
-        line = work[k : k + 1, :] * r
-        work = jnp.where(row == k, line, work - jnp.where(row > k, column, 0.0) * line)
-    return lower[:, :size], work[:, size:]
+        line = inv[k : k + 1, :] * r
+        inv = jnp.where(row == k, line, inv - jnp.where(row > k, column, 0.0) * line)
+    return lower[:, :size], inv[:, :size]
+
+
+def orthonormal(onto, basis, own):
+    count = len(onto)
+    coef = jnp.concatenate(onto, axis=1)
+    lines = []
+    for m in range(count):
+        line = [*basis[m][:m], 0.5 * basis[m][m]] + [jnp.zeros_like(own)] * (count - 1 - m)
+        lines.append(jnp.concatenate(line, axis=1))
+    part = fdot(coef, jnp.concatenate(lines, axis=0)) - coef
+    gram = own + (fdot(part, coef, NT) + fdot(coef, part, NT))
+    lower, inv = factor(gram)
+    return lower, jnp.concatenate([inv, -fdot(inv, coef)], axis=1)
 
 
 def tdot(t, x):
@@ -76,21 +91,6 @@
     size = t.shape[0]
     big = bdot(jnp.concatenate([t_hi, t_lo], axis=0), x_hi)
     return big[:size] + (big[size:] + bdot(t_hi, x_lo))
-
-
-def orthonormal(onto, basis, own):
-    count = len(onto)
-    gram = own
-    for l in range(count):
-        part = -2.0 * onto[l]
-        for m in range(count):
-            if m >= l:
-                part = part + fdot(onto[m], basis[m][l])
-            else:
-                part = part + fdot(onto[m], basis[l][m], NT)
-        gram = gram + fdot(part, onto[l], NT)
-    lower, inv = factor(gram)
-    return lower, jnp.concatenate([inv] + [-fdot(inv, c) for c in onto], axis=1)
 
 
 def added(ref):

time: 199 us -> 193 us (0.970)
  Pallas kernels: 65.5 us -> 59.3 us
    pallas_call x11, Pallas kernels: 65.5 us -> 59.3 us  [call(): pl.pallas_call(kernel, out_shape=tuple(outs), in_specs=[pl.BlockSpec(memo...]
where the time goes in v5:
time: 193 us; the launch traced here: 192 us
  blocking collectives  132 us (68%)
  Pallas kernels  59.3 us (31%)
    all_to_all x9, blocking collectives, exchange(): return lax.all_to_all(value, axis, split_axis=0, concat_axis=0, tiled=True)  132 us
    pallas_call x11, Pallas kernels, call(): pl.pallas_call(kernel, out_shape=tuple(outs), in_specs=[pl.BlockSpec(memo...  59.3 us

profile of v5, /device:TPU:1, one launch (start us, length us, event | category | flops | bytes accessed | tf_op | source)
XLA Modules:
  0.0 192.2 jit_solution(7268529927043831150)
XLA Ops:
  0.6 1.2 shard_map.111
  1.9 28.7 %shard_map.112 = (bf16[1024,4096]{1,0:T(8,128)(2,1)S(1)}, bf16[1024,4096]{1,0:T(8,128)(2,1)S(1)}, bf16[1024,4096]{1,0:T(8,128)(2,1)S(1)}, bf16[1024,4096]{1,0:T(...) custom-call(s32[2,4096]{1,0:T(2,128)S(1)} %get-tuple-element.38.sp_v, ...), custom_call_target="tpu_custom_call" | custom-call | tf_op jit(solution)/shard_map/pallas_call | solution.py:356
  30.6 16.9 %all_to_all.45.rs = f32[16,32,128]{2,1,0:T(8,128)S(1)} all-to-all(f32[16,32,128]{2,1,0:T(8,128)S(1)} %get-tuple-element.45), channel_id=1, replica_groups=mesh['sta'=16,'cel'=16] {'sta'}, dimensions={0} | all-to-all | bytes 524288 | tf_op jit(solution)/shard_map/all_to_all | solution.py:371
  47.5 11.0 %all_to_all.46.ag.ag0 = f32[16,16,128]{2,1,0:T(8,128)S(1)} all-to-all(f32[16,16,128]{2,1,0:T(8,128)S(1)} %get-tuple-element.46), channel_id=1, replica_groups=mesh['sta'=16,'cel'=16] {'sta'}, dimensions={0} | all-to-all | bytes 262144 | tf_op jit(solution)/shard_map/all_to_all | solution.py:371
  58.5 6.7 %shard_map.114 = f32[16,8,1152]{2,1,0:T(8,128)S(1)} custom-call(f32[16,16,128]{2,1,0:T(8,128)S(1)} %all_to_all.46.ag.ag0, f32[16,2048]{1,0:T(8,128)S(1)} %get-tuple-element.47.q.refs_7_, f32[1,2048]{1,0:T(1,128)S(1)} %get-tuple-element.42.rho_v.rho, bf16[1024,4096]{1,0:T(8,128)(2,1)S(1)} %get-tuple-element.48.refs_0_, ...), custom_call_target="tpu_custom_call" | custom-call | tf_op jit(solution)/shard_map/pallas_call | solution.py:356
  65.3 25.4 %all_to_all.47.refs_0_ = f32[16,8,1152]{2,1,0:T(8,128)S(1)} all-to-all(f32[16,8,1152]{2,1,0:T(8,128)S(1)} %shard_map.114), channel_id=1, replica_groups=mesh['sta'=16,'cel'=16] {'cel'}, dimensions={0} | all-to-all | bytes 1179648 | tf_op jit(solution)/shard_map/all_to_all | solution.py:371
  90.7 1.2 shard_map.115
  91.9 11.9 %all_to_all.48.ag.ag1 = f32[16,16,256]{2,1,0:T(8,128)S(1)} all-to-all(f32[16,16,256]{2,1,0:T(8,128)S(1)} %get-tuple-element.52), channel_id=1, replica_groups=mesh['sta'=16,'cel'=16] {'cel'}, dimensions={0} | all-to-all | bytes 524288 | tf_op jit(solution)/shard_map/all_to_all | solution.py:371
  103.8 10.1 %shard_map.116 = f32[16,32,128]{2,1,0:T(8,128)S(1)} custom-call(f32[16,16,256]{2,1,0:T(8,128)S(1)} %all_to_all.48.ag.ag1, bf16[64,4096]{1,0:T(8,128)(2,1)S(1)} %get-tuple-element.53.left_rows, f32[16,128]{1,0:T(8,128)S(1)} %get-tuple-element.54.stats0, f32[1,2048]{1,0:T(1,128)S(1)} %get-tuple-element.42.rho_v.rho, ...), custom_call_target="tpu_custom_call" | custom-call | tf_op jit(solution)/shard_map/pallas_call | solution.py:356
  113.9 15.0 %all_to_all.49.refs_0_ = f32[16,32,128]{2,1,0:T(8,128)S(1)} all-to-all(f32[16,32,128]{2,1,0:T(8,128)S(1)} %shard_map.116), channel_id=1, replica_groups=mesh['sta'=16,'cel'=16] {'sta'}, dimensions={0} | all-to-all | bytes 524288 | tf_op jit(solution)/shard_map/all_to_all | solution.py:371
  129.0 1.1 shard_map.117
  130.1 11.0 %all_to_all.50.ag2.refs_6_ = f32[16,16,128]{2,1,0:T(8,128)S(1)} all-to-all(f32[16,16,128]{2,1,0:T(8,128)S(1)} %get-tuple-element.56), channel_id=1, replica_groups=mesh['sta'=16,'cel'=16] {'sta'}, dimensions={0} | all-to-all | bytes 262144 | tf_op jit(solution)/shard_map/all_to_all | solution.py:371
  141.2 6.0 %shard_map.118 = (f32[16,2048]{1,0:T(8,128)S(1)}, f32[16,128]{1,0:T(8,128)S(1)}, f32[16,8,640]{2,1,0:T(8,128)S(1)}) custom-call(f32[16,16,128]{2,1,0:T(8,128)S(1)} %all_to_all.50.ag2.refs_6_, f32[16,16,128]{2,1,0:T(8,128)S(1)} %all_to_all.46.ag.ag0, f32[16,2048]{1,0:T(8,128)S(1)} %get-tuple-element.47.q.refs_7_, f32[1,2048]{1,0:T(1,128)S(1)} %get-tuple-element.42.rho_v.rho, ...), custom_call_target="tpu_custom_call" | custom-call | tf_op jit(solution)/shard_map/pallas_call | solution.py:356
  147.2 13.8 %all_to_all.51.refs_0_ = f32[16,8,640]{2,1,0:T(8,128)S(1)} all-to-all(f32[16,8,640]{2,1,0:T(8,128)S(1)} %get-tuple-element.59), channel_id=1, replica_groups=mesh['sta'=16,'cel'=16] {'cel'}, dimensions={0} | all-to-all | bytes 655360 | tf_op jit(solution)/shard_map/all_to_all | solution.py:371
  160.9 1.2 shard_map.119
  162.1 13.5 %all_to_all.52.ag3.refs_2_ = f32[16,16,256]{2,1,0:T(8,128)S(1)} all-to-all(f32[16,16,256]{2,1,0:T(8,128)S(1)} %get-tuple-element.62), channel_id=1, replica_groups=mesh['sta'=16,'cel'=16] {'cel'}, dimensions={0} | all-to-all | bytes 524288 | tf_op jit(solution)/shard_map/all_to_all | solution.py:371
  175.6 0.9 shard_map.120
  176.5 13.5 %all_to_all.53.refs_0_ = f32[16,16,128]{2,1,0:T(8,128)S(1)} all-to-all(f32[16,16,128]{2,1,0:T(8,128)S(1)} %get-tuple-element.64), channel_id=1, replica_groups=mesh['sta'=16,'cel'=16] {'sta'}, dimensions={0} | all-to-all | bytes 262144 | tf_op jit(solution)/shard_map/all_to_all | solution.py:371
  190.1 2.1 %shard_map.121 = (f32[2,16,2048]{2,1,0:T(8,128)}, f32[16,4096]{1,0:T(8,128)}, f32[2,16,16]{2,1,0:T(8,128)}, f32[2,16,16]{2,1,0:T(8,128)}) custom-call(f32[16,16,128]{2,1,0:T(8,128)S(1)} %all_to_all.53.refs_0_, f32[16,128]{1,0:T(8,128)S(1)} %get-tuple-element.65.refs_1_, f32[16,16,256]{2,1,0:T(8,128)S(1)} %all_to_all.52.ag3.refs_2_, ...), custom_call_target="tpu_custom_call" | custom-call | tf_op jit(solution)/shard_map/pallas_call | solution.py:356
  (1 shorter events, 0.0 us)

commit v6 on v5

--- a/solution.py
+++ b/solution.py
@@ -189,13 +189,17 @@
 
         lax.fori_loop(0, n_s // (2 * TILE), station_block, 0)
         prepare(jnp.minimum(c0 + TILE, n_c - TILE))
-        big = bdot(rows[...], hi_ref[pl.ds(g0, TILE), :], NT)
-        small = bdot(rows[:32, :], lo_ref[pl.ds(g0, TILE), :], NT)
-        total = (big[:32] + big[32:] + small) * (12.0 * rho_v[0:1, pl.ds(c0, TILE)])
+        total = jnp.zeros((32, TILE), F32)
+        for k in range(n_s // TILE):
+            own = slice(k * TILE, k * TILE + TILE)
+            square[:, own] = bdot(a_ref[...], b_ref[:, own])
+            big = bdot(rows[:, own], hi_ref[pl.ds(g0, TILE), own], NT)
+            small = bdot(rows[:32, own], lo_ref[pl.ds(g0, TILE), own], NT)
+            total = total + (big[:32] + big[32:] + small)
+        total = total * (12.0 * rho_v[0:1, pl.ds(c0, TILE)])
         for k in range(2):
             piece = 2 * cb + k + part * (n_c // PARTS // 128)
             out[piece] = total[:, 128 * k : 128 * k + 128]
-        square[...] = bdot(a_ref[...], b_ref[...])
         return carry
 
     prepare(0)

time: 193 us -> 190 us (0.984)
  Pallas kernels: 59.3 us -> 56.5 us
    pallas_call x11, Pallas kernels: 59.3 us -> 56.5 us  [call(): pl.pallas_call(kernel, out_shape=tuple(outs), in_specs=[pl.BlockSpec(memo...]
where the time goes in v6:
time: 190 us; the launch traced here: 189 us
  blocking collectives  132 us (69%)
  Pallas kernels  56.5 us (30%)
    all_to_all x9, blocking collectives, exchange(): return lax.all_to_all(value, axis, split_axis=0, concat_axis=0, tiled=True)  132 us
    pallas_call x11, Pallas kernels, call(): pl.pallas_call(kernel, out_shape=tuple(outs), in_specs=[pl.BlockSpec(memo...  56.5 us

profile of v6, /device:TPU:1, one launch (start us, length us, event | category | flops | bytes accessed | tf_op | source)
XLA Modules:
  0.0 189.4 jit_solution(16688575308169487371)
XLA Ops:
  0.6 1.2 shard_map.111
  1.9 25.8 %shard_map.112 = (bf16[1024,4096]{1,0:T(8,128)(2,1)S(1)}, bf16[1024,4096]{1,0:T(8,128)(2,1)S(1)}, bf16[1024,4096]{1,0:T(8,128)(2,1)S(1)}, bf16[1024,4096]{1,0:T(...) custom-call(s32[2,4096]{1,0:T(2,128)S(1)} %get-tuple-element.38.sp_v, ...), custom_call_target="tpu_custom_call" | custom-call | tf_op jit(solution)/shard_map/pallas_call | solution.py:360
  27.7 16.9 %all_to_all.45.rs = f32[16,32,128]{2,1,0:T(8,128)S(1)} all-to-all(f32[16,32,128]{2,1,0:T(8,128)S(1)} %get-tuple-element.45), channel_id=1, replica_groups=mesh['sta'=16,'cel'=16] {'sta'}, dimensions={0} | all-to-all | bytes 524288 | tf_op jit(solution)/shard_map/all_to_all | solution.py:375
  44.7 11.0 %all_to_all.46.ag.ag0 = f32[16,16,128]{2,1,0:T(8,128)S(1)} all-to-all(f32[16,16,128]{2,1,0:T(8,128)S(1)} %get-tuple-element.46), channel_id=1, replica_groups=mesh['sta'=16,'cel'=16] {'sta'}, dimensions={0} | all-to-all | bytes 262144 | tf_op jit(solution)/shard_map/all_to_all | solution.py:375
  55.7 6.7 %shard_map.114 = f32[16,8,1152]{2,1,0:T(8,128)S(1)} custom-call(f32[16,16,128]{2,1,0:T(8,128)S(1)} %all_to_all.46.ag.ag0, f32[16,2048]{1,0:T(8,128)S(1)} %get-tuple-element.47.q.refs_7_, f32[1,2048]{1,0:T(1,128)S(1)} %get-tuple-element.42.rho_v.rho, bf16[1024,4096]{1,0:T(8,128)(2,1)S(1)} %get-tuple-element.48.refs_0_, ...), custom_call_target="tpu_custom_call" | custom-call | tf_op jit(solution)/shard_map/pallas_call | solution.py:360
  62.4 25.5 %all_to_all.47.refs_0_ = f32[16,8,1152]{2,1,0:T(8,128)S(1)} all-to-all(f32[16,8,1152]{2,1,0:T(8,128)S(1)} %shard_map.114), channel_id=1, replica_groups=mesh['sta'=16,'cel'=16] {'cel'}, dimensions={0} | all-to-all | bytes 1179648 | tf_op jit(solution)/shard_map/all_to_all | solution.py:375
  87.9 1.2 shard_map.115
  89.1 11.9 %all_to_all.48.ag.ag1 = f32[16,16,256]{2,1,0:T(8,128)S(1)} all-to-all(f32[16,16,256]{2,1,0:T(8,128)S(1)} %get-tuple-element.52), channel_id=1, replica_groups=mesh['sta'=16,'cel'=16] {'cel'}, dimensions={0} | all-to-all | bytes 524288 | tf_op jit(solution)/shard_map/all_to_all | solution.py:375
  101.0 10.1 %shard_map.116 = f32[16,32,128]{2,1,0:T(8,128)S(1)} custom-call(f32[16,16,256]{2,1,0:T(8,128)S(1)} %all_to_all.48.ag.ag1, bf16[64,4096]{1,0:T(8,128)(2,1)S(1)} %get-tuple-element.53.left_rows, f32[16,128]{1,0:T(8,128)S(1)} %get-tuple-element.54.stats0, f32[1,2048]{1,0:T(1,128)S(1)} %get-tuple-element.42.rho_v.rho, ...), custom_call_target="tpu_custom_call" | custom-call | tf_op jit(solution)/shard_map/pallas_call | solution.py:360
  111.1 15.0 %all_to_all.49.refs_0_ = f32[16,32,128]{2,1,0:T(8,128)S(1)} all-to-all(f32[16,32,128]{2,1,0:T(8,128)S(1)} %shard_map.116), channel_id=1, replica_groups=mesh['sta'=16,'cel'=16] {'sta'}, dimensions={0} | all-to-all | bytes 524288 | tf_op jit(solution)/shard_map/all_to_all | solution.py:375
  126.2 1.1 shard_map.117
  127.3 11.0 %all_to_all.50.ag2.refs_6_ = f32[16,16,128]{2,1,0:T(8,128)S(1)} all-to-all(f32[16,16,128]{2,1,0:T(8,128)S(1)} %get-tuple-element.56), channel_id=1, replica_groups=mesh['sta'=16,'cel'=16] {'sta'}, dimensions={0} | all-to-all | bytes 262144 | tf_op jit(solution)/shard_map/all_to_all | solution.py:375
  138.3 6.0 %shard_map.118 = (f32[16,2048]{1,0:T(8,128)S(1)}, f32[16,128]{1,0:T(8,128)S(1)}, f32[16,8,640]{2,1,0:T(8,128)S(1)}) custom-call(f32[16,16,128]{2,1,0:T(8,128)S(1)} %all_to_all.50.ag2.refs_6_, f32[16,16,128]{2,1,0:T(8,128)S(1)} %all_to_all.46.ag.ag0, f32[16,2048]{1,0:T(8,128)S(1)} %get-tuple-element.47.q.refs_7_, f32[1,2048]{1,0:T(1,128)S(1)} %get-tuple-element.42.rho_v.rho, ...), custom_call_target="tpu_custom_call" | custom-call | tf_op jit(solution)/shard_map/pallas_call | solution.py:360
  144.3 13.8 %all_to_all.51.refs_0_ = f32[16,8,640]{2,1,0:T(8,128)S(1)} all-to-all(f32[16,8,640]{2,1,0:T(8,128)S(1)} %get-tuple-element.59), channel_id=1, replica_groups=mesh['sta'=16,'cel'=16] {'cel'}, dimensions={0} | all-to-all | bytes 655360 | tf_op jit(solution)/shard_map/all_to_all | solution.py:375
  158.1 1.2 shard_map.119
  159.3 13.5 %all_to_all.52.ag3.refs_2_ = f32[16,16,256]{2,1,0:T(8,128)S(1)} all-to-all(f32[16,16,256]{2,1,0:T(8,128)S(1)} %get-tuple-element.62), channel_id=1, replica_groups=mesh['sta'=16,'cel'=16] {'cel'}, dimensions={0} | all-to-all | bytes 524288 | tf_op jit(solution)/shard_map/all_to_all | solution.py:375
  172.8 0.9 shard_map.120
  173.7 13.5 %all_to_all.53.refs_0_ = f32[16,16,128]{2,1,0:T(8,128)S(1)} all-to-all(f32[16,16,128]{2,1,0:T(8,128)S(1)} %get-tuple-element.64), channel_id=1, replica_groups=mesh['sta'=16,'cel'=16] {'sta'}, dimensions={0} | all-to-all | bytes 262144 | tf_op jit(solution)/shard_map/all_to_all | solution.py:375
  187.2 2.1 %shard_map.121 = (f32[2,16,2048]{2,1,0:T(8,128)}, f32[16,4096]{1,0:T(8,128)}, f32[2,16,16]{2,1,0:T(8,128)}, f32[2,16,16]{2,1,0:T(8,128)}) custom-call(f32[16,16,128]{2,1,0:T(8,128)S(1)} %all_to_all.53.refs_0_, f32[16,128]{1,0:T(8,128)S(1)} %get-tuple-element.65.refs_1_, f32[16,16,256]{2,1,0:T(8,128)S(1)} %all_to_all.52.ag3.refs_2_, ...), custom_call_target="tpu_custom_call" | custom-call | tf_op jit(solution)/shard_map/pallas_call | solution.py:360
  (1 shorter events, 0.0 us)

commit v7 on v6

--- a/solution.py
+++ b/solution.py
@@ -174,8 +174,8 @@
         c0 = pl.multiple_of(part * (n_c // PARTS) + g0, TILE)
 
         def station_block(sb, inner):
-            for half in range(2):
-                here = pl.ds(pl.multiple_of(sb * 2 * TILE + half * TILE, TILE), TILE)
+            for half in range(4):
+                here = pl.ds(pl.multiple_of(sb * 4 * TILE + half * TILE, TILE), TILE)
                 height = sz_v[:, here]
                 for r0 in range(0, TILE, 8):
                     dz = height + jnp.concatenate([czb[r0 : r0 + 8, :]] * 2, axis=1)
@@ -187,7 +187,7 @@
                     lo_ref[where, here] = (g - hi_ref[where, here].astype(F32)).astype(BF16)
             return inner
 
-        lax.fori_loop(0, n_s // (2 * TILE), station_block, 0)
+        lax.fori_loop(0, n_s // (4 * TILE), station_block, 0)
         prepare(jnp.minimum(c0 + TILE, n_c - TILE))
         total = jnp.zeros((32, TILE), F32)
         for k in range(n_s // TILE):
@@ -215,7 +215,7 @@
 
 
 def forward_product(rows, count, matrix, out, stats):
-    step = 4 * TILE
+    step = 8 * TILE
     size = matrix[0].shape[0]
     tile = wide(stats)
 

time: 190 us -> 189 us (level)
  no operation moved by 1% of the time
where the time goes in v7:
time: 189 us; the launch traced here: 188 us
  blocking collectives  132 us (70%)
  Pallas kernels  55.5 us (29%)
    all_to_all x9, blocking collectives, exchange(): return lax.all_to_all(value, axis, split_axis=0, concat_axis=0, tiled=True)  132 us
    pallas_call x11, Pallas kernels, call(): pl.pallas_call(kernel, out_shape=tuple(outs), in_specs=[pl.BlockSpec(memo...  55.5 us

profile of v7, /device:TPU:1, one launch (start us, length us, event | category | flops | bytes accessed | tf_op | source)
XLA Modules:
  0.0 188.4 jit_solution(17431839432282137117)
XLA Ops:
  0.6 1.2 shard_map.111
  1.9 25.3 %shard_map.112 = (bf16[1024,4096]{1,0:T(8,128)(2,1)S(1)}, bf16[1024,4096]{1,0:T(8,128)(2,1)S(1)}, bf16[1024,4096]{1,0:T(8,128)(2,1)S(1)}, bf16[1024,4096]{1,0:T(...) custom-call(s32[2,4096]{1,0:T(2,128)S(1)} %get-tuple-element.38.sp_v, ...), custom_call_target="tpu_custom_call" | custom-call | tf_op jit(solution)/shard_map/pallas_call | solution.py:360
  27.2 16.9 %all_to_all.45.rs = f32[16,32,128]{2,1,0:T(8,128)S(1)} all-to-all(f32[16,32,128]{2,1,0:T(8,128)S(1)} %get-tuple-element.45), channel_id=1, replica_groups=mesh['sta'=16,'cel'=16] {'sta'}, dimensions={0} | all-to-all | bytes 524288 | tf_op jit(solution)/shard_map/all_to_all | solution.py:375
  44.2 11.0 %all_to_all.46.ag.ag0 = f32[16,16,128]{2,1,0:T(8,128)S(1)} all-to-all(f32[16,16,128]{2,1,0:T(8,128)S(1)} %get-tuple-element.46), channel_id=1, replica_groups=mesh['sta'=16,'cel'=16] {'sta'}, dimensions={0} | all-to-all | bytes 262144 | tf_op jit(solution)/shard_map/all_to_all | solution.py:375
  55.2 6.5 %shard_map.114 = f32[16,8,1152]{2,1,0:T(8,128)S(1)} custom-call(f32[16,16,128]{2,1,0:T(8,128)S(1)} %all_to_all.46.ag.ag0, f32[16,2048]{1,0:T(8,128)S(1)} %get-tuple-element.47.q.refs_7_, f32[1,2048]{1,0:T(1,128)S(1)} %get-tuple-element.42.rho_v.rho, bf16[1024,4096]{1,0:T(8,128)(2,1)S(1)} %get-tuple-element.48.refs_0_, ...), custom_call_target="tpu_custom_call" | custom-call | tf_op jit(solution)/shard_map/pallas_call | solution.py:360
  61.7 25.5 %all_to_all.47.refs_0_ = f32[16,8,1152]{2,1,0:T(8,128)S(1)} all-to-all(f32[16,8,1152]{2,1,0:T(8,128)S(1)} %shard_map.114), channel_id=1, replica_groups=mesh['sta'=16,'cel'=16] {'cel'}, dimensions={0} | all-to-all | bytes 1179648 | tf_op jit(solution)/shard_map/all_to_all | solution.py:375
  87.1 1.2 shard_map.115
  88.4 11.9 %all_to_all.48.ag.ag1 = f32[16,16,256]{2,1,0:T(8,128)S(1)} all-to-all(f32[16,16,256]{2,1,0:T(8,128)S(1)} %get-tuple-element.52), channel_id=1, replica_groups=mesh['sta'=16,'cel'=16] {'cel'}, dimensions={0} | all-to-all | bytes 524288 | tf_op jit(solution)/shard_map/all_to_all | solution.py:375
  100.2 10.1 %shard_map.116 = f32[16,32,128]{2,1,0:T(8,128)S(1)} custom-call(f32[16,16,256]{2,1,0:T(8,128)S(1)} %all_to_all.48.ag.ag1, bf16[64,4096]{1,0:T(8,128)(2,1)S(1)} %get-tuple-element.53.left_rows, f32[16,128]{1,0:T(8,128)S(1)} %get-tuple-element.54.stats0, f32[1,2048]{1,0:T(1,128)S(1)} %get-tuple-element.42.rho_v.rho, ...), custom_call_target="tpu_custom_call" | custom-call | tf_op jit(solution)/shard_map/pallas_call | solution.py:360
  110.4 15.0 %all_to_all.49.refs_0_ = f32[16,32,128]{2,1,0:T(8,128)S(1)} all-to-all(f32[16,32,128]{2,1,0:T(8,128)S(1)} %shard_map.116), channel_id=1, replica_groups=mesh['sta'=16,'cel'=16] {'sta'}, dimensions={0} | all-to-all | bytes 524288 | tf_op jit(solution)/shard_map/all_to_all | solution.py:375
  125.4 1.1 shard_map.117
  126.5 11.0 %all_to_all.50.ag2.refs_6_ = f32[16,16,128]{2,1,0:T(8,128)S(1)} all-to-all(f32[16,16,128]{2,1,0:T(8,128)S(1)} %get-tuple-element.56), channel_id=1, replica_groups=mesh['sta'=16,'cel'=16] {'sta'}, dimensions={0} | all-to-all | bytes 262144 | tf_op jit(solution)/shard_map/all_to_all | solution.py:375
  137.6 5.8 %shard_map.118 = (f32[16,2048]{1,0:T(8,128)S(1)}, f32[16,128]{1,0:T(8,128)S(1)}, f32[16,8,640]{2,1,0:T(8,128)S(1)}) custom-call(f32[16,16,128]{2,1,0:T(8,128)S(1)} %all_to_all.50.ag2.refs_6_, f32[16,16,128]{2,1,0:T(8,128)S(1)} %all_to_all.46.ag.ag0, f32[16,2048]{1,0:T(8,128)S(1)} %get-tuple-element.47.q.refs_7_, f32[1,2048]{1,0:T(1,128)S(1)} %get-tuple-element.42.rho_v.rho, ...), custom_call_target="tpu_custom_call" | custom-call | tf_op jit(solution)/shard_map/pallas_call | solution.py:360
  143.3 13.8 %all_to_all.51.refs_0_ = f32[16,8,640]{2,1,0:T(8,128)S(1)} all-to-all(f32[16,8,640]{2,1,0:T(8,128)S(1)} %get-tuple-element.59), channel_id=1, replica_groups=mesh['sta'=16,'cel'=16] {'cel'}, dimensions={0} | all-to-all | bytes 655360 | tf_op jit(solution)/shard_map/all_to_all | solution.py:375
  157.1 1.2 shard_map.119
  158.3 13.5 %all_to_all.52.ag3.refs_2_ = f32[16,16,256]{2,1,0:T(8,128)S(1)} all-to-all(f32[16,16,256]{2,1,0:T(8,128)S(1)} %get-tuple-element.62), channel_id=1, replica_groups=mesh['sta'=16,'cel'=16] {'cel'}, dimensions={0} | all-to-all | bytes 524288 | tf_op jit(solution)/shard_map/all_to_all | solution.py:375
  171.8 0.9 shard_map.120
  172.7 13.5 %all_to_all.53.refs_0_ = f32[16,16,128]{2,1,0:T(8,128)S(1)} all-to-all(f32[16,16,128]{2,1,0:T(8,128)S(1)} %get-tuple-element.64), channel_id=1, replica_groups=mesh['sta'=16,'cel'=16] {'sta'}, dimensions={0} | all-to-all | bytes 262144 | tf_op jit(solution)/shard_map/all_to_all | solution.py:375
  186.2 2.1 %shard_map.121 = (f32[2,16,2048]{2,1,0:T(8,128)}, f32[16,4096]{1,0:T(8,128)}, f32[2,16,16]{2,1,0:T(8,128)}, f32[2,16,16]{2,1,0:T(8,128)}) custom-call(f32[16,16,128]{2,1,0:T(8,128)S(1)} %all_to_all.53.refs_0_, f32[16,128]{1,0:T(8,128)S(1)} %get-tuple-element.65.refs_1_, f32[16,16,256]{2,1,0:T(8,128)S(1)} %all_to_all.52.ag3.refs_2_, ...), custom_call_target="tpu_custom_call" | custom-call | tf_op jit(solution)/shard_map/pallas_call | solution.py:360
  (1 shorter events, 0.0 us)
